TPU v7x, 256 devices: a whole 4x4x8 slice. The times are simulated.
256 devices in a mesh: gx: 4 (over x), gy: 8 (over y, core), gz: 8 (over z).
Axes of the slice: x: 4, y: 4, z: 8, core: 2. Of those that a mesh axis runs over, the one named last changes fastest.
Arguments:
- ham_blocks: bfloat16 [2048, 128, 128], P(('gx', 'gy', 'gz')), may hold values from -0.119628906 to 0.119628906
- onsite: float32 [256, 768], P(('gx', 'gy', 'gz')), may hold values from -1 to 1
- entry_slot: int32 [256, 36], P(('gx', 'gy', 'gz')), may hold values from 0 to 63, as said below
- send_table: int32 [256, 64, 1], P(('gx', 'gy', 'gz')), may hold values from -1 to 7, as said below
- reads: int32 [256, 8], P(('gx', 'gy', 'gz')), may hold values from 0 to 42, as said below
- gram_targets: int32 [256, 7, 8], P(('gx', 'gy', 'gz')), may hold values from 0 to 36, as said below
- table_pick: int32 [256, 2, 8], P(('gx', 'gy', 'gz')), may hold values from 0 to 3, as said below
- phi: bfloat16 [256, 4, 128, 4096], P(('gx', 'gy', 'gz')), may hold values from -2.390625 to 2.390625
- potential_in: float32 [16, 64, 1024], P('gx', 'gy', 'gz'), may hold values from -1.5 to 1.5
Outputs:
- potential: float32 [16, 64, 1024], P('gx', 'gy', 'gz')
- grid_blocks: float32 [2048, 128, 128], P(('gx', 'gy', 'gz'))
Inputs may be any that keep to these rules, and one draw needn't show every extreme that they name: `entry_slot`: row d holds distinct slot numbers; at most 1 entries of one submatrix come from one device of its plane, and some device gives exactly 1. send_table[o, e, c] is the local block that submatrix e of o's plane reads in slot o's plane number + c, and -1 where e reads no block in that slot. `reads`: 42 marks an unused slot; some brick uses all 8 slots; the number of used slots differs widely between bricks. gram_targets[d, k, r] is 36 where slot r of the brick at face k of d is unused, and an entry below 36 where it is used; one entry of a submatrix receives at most two slots. `table_pick`: the two tables of one slot differ.
All inputs are finite; a program needn't handle non-finite values.
Results may differ from a plain program's by a relative error of at most 0.012.
Values may be sent and summed in bfloat16 or wider, within the bound.
No kernel may reach another device: no remote copies, remote signals or barrier semaphores. Data moves between devices by JAX's collectives and lax.ppermute only.
A program may use at most 128 MiB of HBM per device.

v0:
```python
import functools

import jax
import jax.numpy as jnp
from jax import lax
from jax.experimental import pallas as pl
from jax.experimental.pallas import tpu as pltpu
from jax.sharding import PartitionSpec as P


B = 128
S = 6
M = 768
RMAX = 8
NOV = 4
EPSILON = 1e-06
N = 8
BY = 8
HELD = 8
NEAR = (0, -1, 1, -2, 2)
FAR = (-3, 3, 4)
SIDES = (("gx", 0), ("gy", 1), ("gz", 2))
F32 = jnp.float32
BF16 = jnp.bfloat16

SMEM = pl.BlockSpec(memory_space=pltpu.SMEM)
VMEM = pl.BlockSpec(memory_space=pltpu.VMEM)


def call(kernel, out_shape, ins, smem, scratch=(), limit=24, cost=None):
    return pl.pallas_call(
        kernel,
        out_shape=out_shape,
        in_specs=[SMEM] * smem + [VMEM] * (len(ins) - smem),
        out_specs=jax.tree.map(lambda _: VMEM, out_shape),
        scratch_shapes=list(scratch),
        compiler_params=pltpu.CompilerParams(vmem_limit_bytes=limit * 1024 * 1024),
        cost_estimate=cost,
    )(*ins)


def shape(dims, dtype):
    return jax.ShapeDtypeStruct(dims, dtype)


def wrapped(i):
    return lax.bitwise_and(i, N - 1)


def near_kernel(table_ref, here_ref, *refs):
    out_ref = refs[-1]
    for o, offset in enumerate(NEAR):
        row = wrapped(here_ref[0] + offset)

        def one(j, carry):
            out_ref[j, o] = refs[o][jnp.maximum(table_ref[row, 0, j], 0)]
            return carry

        lax.fori_loop(0, N, one, 0, unroll=2)


def far_kernel(table_ref, here_ref, *refs):
    sets = refs[: len(FAR)]
    own = refs[len(FAR) : len(FAR) + N // 2]
    other_ref = refs[len(FAR) + N // 2]
    for o, offset in enumerate(FAR):
        row = wrapped(here_ref[0] + offset)
        for step in range(N // 2):
            y = wrapped(here_ref[1] + 2 * step)
            own[step][o] = sets[o][jnp.maximum(table_ref[row, 0, y], 0)]
            other = jnp.maximum(table_ref[row, 0, y ^ 1], 0)
            other_ref[step * len(FAR) + o] = sets[o][other]


def density_kernel(slots_ref, here_ref, *refs):
    near_ref = refs[0]
    far = refs[1 : 1 + N // 2]
    onsite_ref, v_ref, out_ref, incoming_ref, h_ref, x_ref, q_ref = refs[1 + N // 2 :]
    for o, offset in enumerate(NEAR):

        def keep(i, carry):
            incoming_ref[(offset % N) * N + i] = near_ref[i, o]
            return carry

        lax.fori_loop(0, N, keep, 0, unroll=2)
    for step in range(N // 2):
        i = wrapped(here_ref[1] - 2 * step)
        for o, offset in enumerate(FAR):
            incoming_ref[(offset % N) * N + i] = far[step][o]
            incoming_ref[(offset % N) * N + (i ^ 1)] = far[step][len(FAR) + o]
    v = v_ref[...]
    high = v.astype(BF16)
    rest = v - high.astype(F32)
    middle = rest.astype(BF16)
    low = (rest - middle.astype(F32)).astype(BF16)
    out_ref[S] = jnp.concatenate([high, middle, low, jnp.zeros_like(low)], axis=0)
    rows = lax.broadcasted_iota(jnp.int32, (B, B), 0)
    cols = lax.broadcasted_iota(jnp.int32, (B, B), 1)
    eye = rows == cols
    total = jnp.zeros((8, B), F32)

    def block(s, t):
        slot = slots_ref[s * S + t]
        offset = wrapped(slot - here_ref[0])
        return incoming_ref[offset * N + lax.div(slot, N)].astype(F32)

    for s in range(S):
        for t in range(s, S):
            if s == t:
                a = block(s, s)
                diag = onsite_ref[0:1, s * B : (s + 1) * B]
                h = 0.5 * (a + a.T) + jnp.where(eye, diag, 0.0)
                h_ref[s * B : (s + 1) * B, s * B : (s + 1) * B] = h
                total = total + jnp.sum((h * h).reshape(B // 8, 8, B), axis=0)
            else:
                h = 0.5 * (block(s, t) + block(t, s).T)
                h_ref[s * B : (s + 1) * B, t * B : (t + 1) * B] = h
                h_ref[t * B : (t + 1) * B, s * B : (s + 1) * B] = h.T
                total = total + 2.0 * jnp.sum((h * h).reshape(B // 8, 8, B), axis=0)
    norm = jnp.sum(jnp.sum(total, axis=0, keepdims=True), axis=1, keepdims=True)
    factor = lax.rsqrt(norm / M + EPSILON) / 1.3

    def scaled(s, carry):
        part = pl.ds(pl.multiple_of(s * B, B), B)
        x_ref[part, :] = (h_ref[part, :] * factor).astype(BF16)
        return carry

    lax.fori_loop(0, S, scaled, 0)
    x0 = x_ref[...]
    for s in range(0, S, 2):
        part = slice(s * B, (s + 2) * B)
        q_ref[:, part] = jnp.dot(x0, x_ref[:, part], preferred_element_type=F32).astype(BF16)
    for s in range(0, S, 2):
        part = slice(s * B, (s + 2) * B)
        cube = jnp.dot(x0, q_ref[:, part], preferred_element_type=F32)
        h_ref[:, part] = 1.5 * x_ref[:, part].astype(F32) - 0.5 * cube
    x1 = h_ref[...].astype(BF16)
    column = x1[:, :B]
    inner = jnp.dot(x1, column, preferred_element_type=F32).astype(BF16)
    outer = jnp.dot(x1, inner, preferred_element_type=F32)
    for s in range(S):
        part = slice(s * B, (s + 1) * B)
        value = 1.5 * column[part].astype(F32) - 0.5 * outer[part]
        if s == 0:
            value = jnp.where(eye, 1.0, 0.0) - value
        else:
            value = 0.0 - value
        out_ref[s] = (0.5 * value).astype(BF16)


def hold_kernel(phi_ref, out_ref):
    out_ref[...] = phi_ref[...]


def turn_kernel(picks_ref, out_ref):
    def one(j, carry):
        for z in range(N):
            out_ref[z, 0, j] = picks_ref[j * N + z]
        return carry

    lax.fori_loop(0, N, one, 0)


def rho_kernel(reads_ref, pick_ref, *refs):
    faces = refs[:7]
    v_ref, phi_ref, rho_ref, next_ref, p_ref = refs[7:]
    width = 512
    chunks = phi_ref.shape[1] // width
    p_ref[...] = jnp.zeros(p_ref.shape, F32)

    def slot(r, carry):
        code = reads_ref[r]
        row = pl.multiple_of(pick_ref[r] * B, B)
        right = pick_ref[RMAX + r]
        for k in range(7):

            @pl.when((code >= k * S) & (code < (k + 1) * S))
            def _():
                at = (right, pl.ds(row, B))
                p_ref[at] = p_ref[at] + faces[k][code - k * S].astype(F32)

        return carry

    lax.fori_loop(0, RMAX, slot, 0)
    pc = jnp.concatenate([p_ref[t].astype(BF16) for t in range(NOV)], axis=1)

    def some(i, carry):
        for c in range(2):
            c = i * 2 + c
            part = phi_ref[:, pl.ds(pl.multiple_of(c * width, width), width)]
            mixed = jnp.dot(pc, part, preferred_element_type=F32)
            value = mixed * part.astype(F32)
            value = jnp.sum(value.reshape(NOV * B // 8, 8, width), axis=0)
            value = jnp.sum(value, axis=0, keepdims=True)
            for k in range(width // B):
                rho_ref[pl.ds(c * (width // B) + k, 1), :] = value[:, k * B : (k + 1) * B]
        return carry

    lax.fori_loop(0, chunks // 2, some, 0)
    v = v_ref[...]
    count = v.shape[0]

    def field(k):
        terms = [faces[k][S, t * count : (t + 1) * count].astype(F32) for t in range(3)]
        return (terms[0] + terms[1]) + terms[2]

    row = lax.broadcasted_iota(jnp.int32, v.shape, 0)
    lane = lax.broadcasted_iota(jnp.int32, v.shape, 1)
    at_y = lax.rem(row, BY)
    beside = jnp.concatenate([v[BY:], field(2)[:BY]], axis=0)
    beside = beside + jnp.concatenate([field(1)[count - BY :], v[: count - BY]], axis=0)
    beside = beside + jnp.where(
        at_y == BY - 1, pltpu.roll(field(4), BY - 1, 0), pltpu.roll(v, count - 1, 0)
    )
    beside = beside + jnp.where(
        at_y == 0, pltpu.roll(field(3), count - BY + 1, 0), pltpu.roll(v, 1, 0)
    )
    beside = beside + jnp.where(
        lane == B - 1, pltpu.roll(field(6), B - 1, 1), pltpu.roll(v, B - 1, 1)
    )
    beside = beside + jnp.where(lane == 0, pltpu.roll(field(5), 1, 1), pltpu.roll(v, 1, 1))
    next_ref[...] = (beside + rho_ref[...]) / 6.0


def gram_kernel(pick_ref, v_ref, phi_ref, out_ref, w_ref, g_ref):
    for k in range(v_ref.shape[0]):
        part = slice(k * B, (k + 1) * B)
        w_ref[:, part] = (phi_ref[:, part].astype(F32) * v_ref[k : k + 1, :]).astype(BF16)
    for t in range(0, NOV, 2):
        g = lax.dot_general(
            phi_ref[...],
            w_ref[t * B : (t + 2) * B, :],
            (((1,), (1,)), ((), ())),
            preferred_element_type=F32,
        )
        g_ref[t] = g[:, :B]
        g_ref[t + 1] = g[:, B:]

    def slot(r, carry):
        row = pl.multiple_of(pick_ref[r] * B, B)
        out_ref[r] = g_ref[pick_ref[RMAX + r], pl.ds(row, B)].astype(BF16)
        return carry

    lax.fori_loop(0, RMAX, slot, 0)


def return_kernel(targets_ref, slots_ref, here_ref, *refs):
    faces = refs[:7]
    near_ref = refs[7]
    far = refs[8 : 8 + N]
    sum_ref = refs[8 + N]

    def clear(q, carry):
        sum_ref[q] = jnp.zeros((B, B), BF16)
        return carry

    lax.fori_loop(0, sum_ref.shape[0], clear, 0, unroll=8)
    for k in range(7):

        def slot(r, carry):
            target = targets_ref[k * RMAX + r]

            @pl.when(target < S * S)
            def _():
                slot_id = slots_ref[target]
                offset = wrapped(slot_id - here_ref[0])
                at = offset * N + lax.div(slot_id, N)
                total = sum_ref[at].astype(F32) + faces[k][r].astype(F32)
                sum_ref[at] = total.astype(BF16)

            return carry

        lax.fori_loop(0, RMAX, slot, 0)
    for o, offset in enumerate(NEAR):

        def keep(i, carry):
            near_ref[i, o] = sum_ref[(offset % N) * N + i]
            return carry

        lax.fori_loop(0, N, keep, 0, unroll=2)
    for step in range(N):
        i = wrapped(here_ref[1] + step)
        for o, offset in enumerate(FAR):
            far[step][o] = sum_ref[(offset % N) * N + i]


def add_near(acc_ref, table_ref, row, near_ref, o):
    def one(j, carry):
        pick = table_ref[row, 0, j]

        @pl.when(pick >= 0)
        def _():
            acc_ref[pick] = acc_ref[pick] + near_ref[j, o].astype(F32)

        return carry

    lax.fori_loop(0, N, one, 0)


def add_far(acc_ref, table_ref, here_ref, far, o):
    row = wrapped(here_ref[0] + FAR[o])
    for step in range(N):
        pick = table_ref[row, 0, wrapped(here_ref[1] - step)]

        @pl.when(pick >= 0)
        def _():
            acc_ref[pick] = acc_ref[pick] + far[step][o].astype(F32)


def farthest_kernel(table_ref, here_ref, *refs):
    far = refs[:N]
    up_ref, acc_ref = refs[N:]
    acc_ref[...] = jnp.zeros(acc_ref.shape, F32)
    add_far(acc_ref, table_ref, here_ref, far, 2)
    up_ref[...] = acc_ref[...].astype(BF16)


def far_stage_kernel(o, table_ref, here_ref, *refs):
    far = refs[:N]
    next_ref, acc_ref = refs[-2:]
    if len(refs) > N + 2:
        acc_ref[...] = refs[N][...].astype(F32)
    else:
        acc_ref[...] = jnp.zeros(acc_ref.shape, F32)
    add_far(acc_ref, table_ref, here_ref, far, o)
    next_ref[...] = acc_ref[...].astype(BF16)


def near_stage_kernel(o, table_ref, here_ref, near_ref, handed_ref, next_ref, acc_ref):
    acc_ref[...] = handed_ref[...].astype(F32)
    add_near(acc_ref, table_ref, wrapped(here_ref[0] + NEAR[o]), near_ref, o)
    next_ref[...] = acc_ref[...].astype(BF16)


def owner_kernel(table_ref, here_ref, near_ref, up_ref, down_ref, out_ref):
    out_ref[...] = up_ref[...].astype(F32) + down_ref[...].astype(F32)
    add_near(out_ref, table_ref, here_ref[0], near_ref, 0)


def face_exchange(x):
    out = [x]
    for axis, _ in SIDES:
        size = lax.axis_size(axis)
        up = [(i, (i + 1) % size) for i in range(size)]
        out.append(lax.ppermute(x, axis, up))
        out.append(lax.ppermute(x, axis, [(b, a) for a, b in up]))
    return out


def extended(x):
    edges = {}
    for axis, dim in SIDES:
        size, length = (lax.axis_size(axis), x.shape[dim])
        up = [(i, (i + 1) % size) for i in range(size)]
        last = lax.slice_in_dim(x, length - 1, length, axis=dim)
        first = lax.slice_in_dim(x, 0, 1, axis=dim)
        edges[dim] = (
            lax.ppermute(last, axis, up),
            lax.ppermute(first, axis, [(b, a) for a, b in up]),
        )
    done = []
    for _, dim in SIDES:
        low, high = edges[dim]
        around = [(1, 1) if d in done else (0, 0) for d in range(x.ndim)]
        x = jnp.concatenate([jnp.pad(low, around), x, jnp.pad(high, around)], axis=dim)
        done.append(dim)
    return x


def jacobi_step(padded, source):
    beside_all = padded[2:, 1:-1, 1:-1] + padded[:-2, 1:-1, 1:-1]
    beside_all = beside_all + padded[1:-1, 2:, 1:-1] + padded[1:-1, :-2, 1:-1]
    beside_all = beside_all + padded[1:-1, 1:-1, 2:] + padded[1:-1, 1:-1, :-2]
    return (beside_all + source) / 6.0


FAR_OUT = (shape((len(FAR), B, B), BF16),) * (N // 2)
FAR_OUT = FAR_OUT + (shape((N // 2 * len(FAR), B, B), BF16),)


def density_of(slots, here, near, far, onsite, field):
    return call(
        density_kernel,
        shape((S + 1, B, B), BF16),
        (slots, here, near, *far, onsite, field),
        2,
        (
            pltpu.VMEM((N * N, B, B), BF16),
            pltpu.VMEM((M, M), F32),
            pltpu.VMEM((M, M), BF16),
            pltpu.VMEM((M, M), BF16),
        ),
    )


def rho_of(codes, pick, faces, field, tables):
    flat = (tables.shape[1] // B, B)
    out = (shape(flat, F32), shape(flat, F32))
    ins = (codes, pick, *faces, field, tables)
    return call(rho_kernel, out, ins, 2, (pltpu.VMEM((NOV, NOV * B, B), F32),))


def gram_of(pick, potential, tables):
    return call(
        gram_kernel,
        shape((RMAX, B, B), BF16),
        (pick, potential, tables),
        1,
        (pltpu.VMEM(tables.shape, BF16), pltpu.VMEM((NOV, NOV * B, B), F32)),
    )


def returned_of(targets, slots, here, grams):
    out = (shape((N, len(NEAR), B, B), BF16),) + (shape((len(FAR), B, B), BF16),) * N
    ins = (targets, slots, here, *grams)
    out = call(return_kernel, out, ins, 3, (pltpu.VMEM((N * N, B, B), BF16),))
    return out[0], out[1:]


def ring(step):
    size = lax.axis_size("gz")
    return [(i, (i + step) % size) for i in range(size)]


def both_ways(up, down):
    return (lax.ppermute(up, "gz", ring(1)), lax.ppermute(down, "gz", ring(-1)))


def across(x):
    return lax.all_to_all(x, "gy", split_axis=0, concat_axis=0, tiled=True)


def hand_over(far):
    size = lax.axis_size("gy")
    swapped = lax.ppermute(far[-1], "gy", [(i, i ^ 1) for i in range(size)])
    out = []
    for step, own in enumerate(far[:-1]):
        both = jnp.concatenate([own, swapped[step * len(FAR) : (step + 1) * len(FAR)]])
        if step:
            pairs = [(i, (i + 2 * step) % size) for i in range(size)]
            both = lax.ppermute(both, "gy", pairs)
        out.append(both)
    return out


def hand_back(far):
    size = lax.axis_size("gy")
    out = [far[0]]
    for step in range(1, size):
        out.append(lax.ppermute(far[step], "gy", [(i, (i + step) % size) for i in range(size)]))
    return out


def fetched(table, here, ham_blocks):
    up1, down1 = both_ways(ham_blocks, ham_blocks)
    up2, down2 = both_ways(up1, down1)
    up3, down3 = both_ways(up2, down2)
    up4 = lax.ppermute(up3, "gz", ring(1))
    ins = (table, here, ham_blocks, up1, down1, up2, down2)
    near = call(near_kernel, shape((N, len(NEAR), B, B), BF16), ins, 2)
    near = across(near)
    ins = (table, here, up3, down3, up4)
    far = call(far_kernel, FAR_OUT, ins, 2)
    far = hand_over(far)
    return near, far


def brought_back(table, here, near, far):
    acc = (pltpu.VMEM((HELD, B, B), F32),)
    whole = shape((HELD, B, B), BF16)
    far = hand_back(far)
    near = across(near)
    up = call(farthest_kernel, whole, (table, here, *far), 2, acc)
    up = lax.ppermute(up, "gz", ring(1))
    down = call(functools.partial(far_stage_kernel, 0), whole, (table, here, *far), 2, acc)
    kernel = functools.partial(far_stage_kernel, 1)
    up = call(kernel, whole, (table, here, *far, up), 2, acc)
    for stage in (2, 1):
        up, down = both_ways(up, down)
        kernel = functools.partial(near_stage_kernel, 2 * stage)
        up = call(kernel, whole, (table, here, near, up), 2, acc)
        kernel = functools.partial(near_stage_kernel, 2 * stage - 1)
        down = call(kernel, whole, (table, here, near, down), 2, acc)
    up, down = both_ways(up, down)
    ins = (table, here, near, up, down)
    return call(owner_kernel, shape((HELD, B, B), F32), ins, 2)


def shards(
    ham_blocks, onsite, entry_slot, send_table, reads, gram_targets, table_pick, phi, potential_in
):
    slot_ids = entry_slot[0]
    pick = table_pick.reshape(-1)
    tables = phi.reshape(NOV * B, -1)
    tables = call(hold_kernel, shape(tables.shape, BF16), (tables,), 0)
    field = potential_in.reshape(-1, B)
    here = jnp.stack([lax.axis_index("gz"), lax.axis_index("gy")]).astype(jnp.int32)
    sent = pl.pallas_call(
        turn_kernel, out_shape=shape((N, 1, N), jnp.int32), in_specs=[SMEM], out_specs=SMEM
    )(send_table.reshape(-1))
    table = lax.all_to_all(sent, "gz", split_axis=0, concat_axis=0, tiled=True)
    near, far = fetched(table, here, ham_blocks)
    density = density_of(slot_ids, here, near, far, onsite, field)
    faces = face_exchange(density)
    source, first = rho_of(reads[0], pick, faces, field, tables)
    dims = potential_in.shape
    potential = jacobi_step(extended(first.reshape(dims)), source.reshape(dims))
    grams = gram_of(pick, potential.reshape(-1, B), tables)
    near, far = returned_of(gram_targets.reshape(-1), slot_ids, here, face_exchange(grams))
    return (potential, brought_back(table, here, near, far))


def solution(mesh):
    whole = ("gx", "gy", "gz")
    placed = (
        P(whole, None, None),
        P(whole, None),
        P(whole, None),
        P(whole, None, None),
        P(whole, None),
        P(whole, None, None),
        P(whole, None, None),
        P(whole, None, None, None),
        P("gx", "gy", "gz"),
    )
    return jax.shard_map(
        shards,
        mesh=mesh,
        in_specs=placed,
        out_specs=(P("gx", "gy", "gz"), P(whole, None, None)),
        check_vma=False,
    )
```

profile of v0, /device:TPU:1, one launch (start us, length us, event | category | flops | bytes accessed | tf_op | source)
XLA Modules:
  0.0 207.9 jit_solution(7534452359862349290)
XLA Ops:
  3.2 4.0 %collective-permute-start.1 = (bf16[8,128,128]{2,1,0:T(8,128)(2,1)}, bf16[8,128,128]{2,1,0:T(8,128)(2,1)S(1)}, u32[]{:S(2)}, u32[]{:S(2)}) collective-permute-start(bf16[8,128,128]{2,1,0:T(8,128)(2,1)} %refs_0_.1), channel_id=1, source_target_pairs={{0,7},{1,0},{2,1},{3,2},{4,3},{5,4},{6,5},{7,6},{8,15},{9,8},{10,9... | collective-permute-start | bytes 786440 | tf_op jit(solution)/shard_map/ppermute | solution.py:426
  7.2 6.1 %collective-permute-done.refs_1_ = bf16[8,128,128]{2,1,0:T(8,128)(2,1)S(1)} collective-permute-done((bf16[8,128,128]{2,1,0:T(8,128)(2,1)}, bf16[8,128,128]{2,1,0:T(8,128)(2,1)S(1)}, u32[]{:S(2)}, u32[]{:S(2)}) %collective-permute-start) | collective-permute-done | bytes 262176 | tf_op jit(solution)/shard_map/ppermute | solution.py:426
  16.0 5.1 %collective-permute-done.2.refs_3_ = bf16[8,128,128]{2,1,0:T(8,128)(2,1)S(1)} collective-permute-done((bf16[8,128,128]{2,1,0:T(8,128)(2,1)S(1)}, bf16[8,128,128]{2,1,0:T(8,128)(2,1)S(1)}, u32[]{:S(2)}, u32[]{:S(2)}) %collective-permute-start.2) | collective-permute-done | bytes 262176 | tf_op jit(solution)/shard_map/ppermute | solution.py:426
  23.8 4.3 %collective-permute-done.4.refs_0_ = bf16[8,128,128]{2,1,0:T(8,128)(2,1)S(1)} collective-permute-done((bf16[8,128,128]{2,1,0:T(8,128)(2,1)S(1)}, bf16[8,128,128]{2,1,0:T(8,128)(2,1)S(1)}, u32[]{:S(2)}, u32[]{:S(2)}) %collective-permute-start.4) | collective-permute-done | bytes 262176 | tf_op jit(solution)/shard_map/ppermute | solution.py:426
  29.5 4.5 %all-to-all-start = ((s32[8,1,8]{2,1,0:T(1,128)}), s32[8,1,8]{2,1,0:T(1,128)S(1)}, u32[]{:S(2)}, u32[]{:S(2)}) async-start(s32[8,1,8]{2,1,0:T(1,128)} %shard_map.104), calls=%async_computation | async-start | bytes 8192 | tf_op jit(solution)/shard_map/all_to_all | solution.py:501
  34.1 6.4 %all-to-all-done.table_ref = s32[8,1,8]{2,1,0:T(1,128)S(1)} async-done(((s32[8,1,8]{2,1,0:T(1,128)}), s32[8,1,8]{2,1,0:T(1,128)S(1)}, u32[]{:S(2)}, u32[]{:S(2)}) %all-to-all-start) | async-done | bytes 288 | tf_op jit(solution)/shard_map/all_to_all | solution.py:501
  41.2 5.3 %collective-permute-start.7 = (bf16[12,128,128]{2,1,0:T(8,128)(2,1)S(1)}, bf16[12,128,128]{2,1,0:T(8,128)(2,1)S(1)}, u32[]{:S(2)}, u32[]{:S(2)}) collective-permute-start(bf16[12,128,128]{2,1,0:T(8,128)(2,1)S(1)} %get-tuple-element.19), channel_id=1, source_target_pairs={{0,8},{8,0},{16,24},{24,16},{32,40},{40,32},{48,56},{56,48},{1,9},... | collective-permute-start | bytes 1179656 | tf_op jit(solution)/shard_map/ppermute | solution.py:435
  49.4 4.6 %all-to-all-start.1 = ((bf16[8,5,128,128]{3,2,1,0:T(8,128)(2,1)}), bf16[8,5,128,128]{3,2,1,0:T(8,128)(2,1)S(1)}, u32[]{:S(2)}, u32[]{:S(2)}) async-start(bf16[8,5,128,128]{3,2,1,0:T(8,128)(2,1)} %shard_map.105), calls=%async_computation.1 | async-start | bytes 2621440 | tf_op jit(solution)/shard_map/all_to_all | solution.py:430
  58.1 16.4 %collective-permute-done.10.refs_4_ = bf16[6,128,128]{2,1,0:T(8,128)(2,1)S(1)} collective-permute-done((bf16[6,128,128]{2,1,0:T(8,128)(2,1)S(1)}, bf16[6,128,128]{2,1,0:T(8,128)(2,1)S(1)}, u32[]{:S(2)}, u32[]{:S(2)}) %collective-permute-start.10) | collective-permute-done | bytes 196640 | tf_op jit(solution)/shard_map/ppermute | solution.py:441
  76.0 4.1 %collective-permute-done.8.refs_2_ = bf16[6,128,128]{2,1,0:T(8,128)(2,1)S(1)} collective-permute-done((bf16[6,128,128]{2,1,0:T(8,128)(2,1)S(1)}, bf16[6,128,128]{2,1,0:T(8,128)(2,1)S(1)}, u32[]{:S(2)}, u32[]{:S(2)}) %collective-permute-start.8) | collective-permute-done | bytes 196640 | tf_op jit(solution)/shard_map/ppermute | solution.py:441
  80.1 4.9 %shard_map.107.refs_0_ = bf16[7,128,128]{2,1,0:T(8,128)(2,1)S(1)} custom-call(s32[36]{0:T(128)S(1)} %bitcast.25, s32[2]{0:T(128)S(1)} %pad_add_fusion.here_ref, bf16[8,5,128,128]{3,2,1,0:T(8,128)(2,1)S(1)} %all-to-all-done.1.refs_0_, bf16[6,128,128]{2,1,0:T(8,128)(2,1)S(1)} %pad_maximum_fusion.refs_1_, ...), custom_call_target="tpu_custom_call" | custom-call | tf_op jit(solution)/shard_map/pallas_call | solution.py:31
  100.6 4.1 %shard_map.109 = (f32[32,128]{1,0:T(8,128)S(1)}, f32[32,128]{1,0:T(8,128)S(1)}) custom-call(s32[8]{0:T(128)S(1)} %bitcast.27, s32[16]{0:T(128)S(1)} %reshape.30.pick_ref, bf16[7,128,128]{2,1,0:T(8,128)(2,1)S(1)} %shard_map.107.refs_0_, bf16[7,128,128]{2,1,0:T(8,128)(2,1)S(1)} %collective-permute-done.11.refs_1_, ...), custom_call_target="tpu_custom_call" | custom-call | tf_op jit(solution)/shard_map/pallas_call | solution.py:31
  106.2 3.1 %collective-permute-start.19 = (f32[4,1,128]{2,1,0:T(1,128)S(1)}, f32[4,1,128]{2,1,0:T(1,128)S(1)}, u32[]{:S(2)}, u32[]{:S(2)}) collective-permute-start(f32[4,1,128]{2,1,0:T(1,128)S(1)} %get-tuple-element.43), channel_id=1, source_target_pairs={{8,0},{16,8},{24,16},{32,24},{40,32},{48,40},{56,48},{0,56},{9,1},... | collective-permute-start | bytes 6152 | tf_op jit(solution)/shard_map/ppermute | solution.py:359
  114.9 3.4 %shard_map.110.refs_0_ = bf16[8,128,128]{2,1,0:T(8,128)(2,1)S(1)} custom-call(s32[16]{0:T(128)S(1)} %reshape.30.pick_ref, f32[32,128]{1,0:T(8,128)S(1)} %fusion.12.v_ref, bf16[512,4096]{1,0:T(8,128)(2,1)S(1)} %copy-done.2), custom_call_target="tpu_custom_call" | custom-call | tf_op jit(solution)/shard_map/pallas_call | solution.py:31
  131.2 3.2 %shard_map.111 = (bf16[8,5,128,128]{3,2,1,0:T(8,128)(2,1)}, bf16[3,128,128]{2,1,0:T(8,128)(2,1)S(1)}, bf16[3,128,128]{2,1,0:T(8,128)(2,1)S(1)}, bf16[3,128,128]{...) custom-call(s32[56]{0:T(128)S(1)} %reshape.36.targets_ref, ...), custom_call_target="tpu_custom_call" | custom-call | tf_op jit(solution)/shard_map/pallas_call | solution.py:31
  134.4 9.3 %all-to-all-start.2 = ((bf16[8,5,128,128]{3,2,1,0:T(8,128)(2,1)}), bf16[8,5,128,128]{3,2,1,0:T(8,128)(2,1)S(1)}, u32[]{:S(2)}, u32[]{:S(2)}) async-start(bf16[8,5,128,128]{3,2,1,0:T(8,128)(2,1)} %get-tuple-element.25), calls=%async_computation.2 | async-start | bytes 2621440 | tf_op jit(solution)/shard_map/all_to_all | solution.py:430
  150.3 10.1 %collective-permute-done.29.refs_1_ = bf16[3,128,128]{2,1,0:T(8,128)(2,1)S(1)} collective-permute-done((bf16[3,128,128]{2,1,0:T(8,128)(2,1)S(1)}, bf16[3,128,128]{2,1,0:T(8,128)(2,1)S(1)}, u32[]{:S(2)}, u32[]{:S(2)}) %collective-permute-start.29) | collective-permute-done | bytes 98336 | tf_op jit(solution)/shard_map/ppermute | solution.py:450
  166.2 3.5 %collective-permute-done.32.refs_4_ = bf16[3,128,128]{2,1,0:T(8,128)(2,1)S(1)} collective-permute-done((bf16[3,128,128]{2,1,0:T(8,128)(2,1)S(1)}, bf16[3,128,128]{2,1,0:T(8,128)(2,1)S(1)}, u32[]{:S(2)}, u32[]{:S(2)}) %collective-permute-start.32) | collective-permute-done | bytes 98336 | tf_op jit(solution)/shard_map/ppermute | solution.py:450
  174.6 5.3 %collective-permute-done.36.refs_8_ = bf16[8,128,128]{2,1,0:T(8,128)(2,1)S(1)} collective-permute-done((bf16[8,128,128]{2,1,0:T(8,128)(2,1)S(1)}, bf16[8,128,128]{2,1,0:T(8,128)(2,1)S(1)}, u32[]{:S(2)}, u32[]{:S(2)}) %collective-permute-start.36) | collective-permute-done | bytes 262176 | tf_op jit(solution)/shard_map/ppermute | solution.py:474
  181.7 3.2 %collective-permute-start.41 = (bf16[8,128,128]{2,1,0:T(8,128)(2,1)S(1)}, bf16[8,128,128]{2,1,0:T(8,128)(2,1)S(1)}, u32[]{:S(2)}, u32[]{:S(2)}) collective-permute-start(bf16[8,128,128]{2,1,0:T(8,128)(2,1)S(1)} %shard_map.117), channel_id=1, source_target_pairs={{0,7},{1,0},{2,1},{3,2},{4,3},{5,4},{6,5},{7,6},{8,15},{9,8},{10,9... | collective-permute-start | bytes 786440 | tf_op jit(solution)/shard_map/ppermute | solution.py:426
  184.8 4.7 %collective-permute-done.37.handed_ref = bf16[8,128,128]{2,1,0:T(8,128)(2,1)S(1)} collective-permute-done((bf16[8,128,128]{2,1,0:T(8,128)(2,1)S(1)}, bf16[8,128,128]{2,1,0:T(8,128)(2,1)S(1)}, u32[]{:S(2)}, u32[]{:S(2)}) %collective-permute-start.37) | collective-permute-done | bytes 262176 | tf_op jit(solution)/shard_map/ppermute | solution.py:426
  191.3 3.1 %collective-permute-start.42 = (bf16[8,128,128]{2,1,0:T(8,128)(2,1)S(1)}, bf16[8,128,128]{2,1,0:T(8,128)(2,1)S(1)}, u32[]{:S(2)}, u32[]{:S(2)}) collective-permute-start(bf16[8,128,128]{2,1,0:T(8,128)(2,1)S(1)} %shard_map.118), channel_id=1, source_target_pairs={{0,7},{1,0},{2,1},{3,2},{4,3},{5,4},{6,5},{7,6},{8,15},{9,8},{10,9... | collective-permute-start | bytes 786440 | tf_op jit(solution)/shard_map/ppermute | solution.py:426
  194.4 3.9 %collective-permute-done.38.handed_ref = bf16[8,128,128]{2,1,0:T(8,128)(2,1)S(1)} collective-permute-done((bf16[8,128,128]{2,1,0:T(8,128)(2,1)S(1)}, bf16[8,128,128]{2,1,0:T(8,128)(2,1)S(1)}, u32[]{:S(2)}, u32[]{:S(2)}) %collective-permute-start.38) | collective-permute-done | bytes 262176 | tf_op jit(solution)/shard_map/ppermute | solution.py:426
  200.0 6.3 %collective-permute-done.39.up_ref = bf16[8,128,128]{2,1,0:T(8,128)(2,1)S(1)} collective-permute-done((bf16[8,128,128]{2,1,0:T(8,128)(2,1)S(1)}, bf16[8,128,128]{2,1,0:T(8,128)(2,1)S(1)}, u32[]{:S(2)}, u32[]{:S(2)}) %collective-permute-start.39) | collective-permute-done | bytes 262176 | tf_op jit(solution)/shard_map/ppermute | solution.py:426
  (122 shorter events, 78.0 us)
Async XLA Ops:
  0.6 12.7 %collective-permute-start = (bf16[8,128,128]{2,1,0:T(8,128)(2,1)}, bf16[8,128,128]{2,1,0:T(8,128)(2,1)S(1)}, u32[]{:S(2)}, u32[]{:S(2)}) collective-permute-start(bf16[8,128,128]{2,1,0:T(8,128)(2,1)} %refs_0_.1), channel_id=1, source_target_pairs={{0,1},{1,2},{2,3},{3,4},{4,5},{5,6},{6,7},{7,0},{8,9},{9,10},{10,1... | collective-permute-start | bytes 786440 | tf_op jit(solution)/shard_map/ppermute | solution.py:426
  3.2 10.2 %collective-permute-start.1 = (bf16[8,128,128]{2,1,0:T(8,128)(2,1)}, bf16[8,128,128]{2,1,0:T(8,128)(2,1)S(1)}, u32[]{:S(2)}, u32[]{:S(2)}) collective-permute-start(bf16[8,128,128]{2,1,0:T(8,128)(2,1)} %refs_0_.1), channel_id=1, source_target_pairs={{0,7},{1,0},{2,1},{3,2},{4,3},{5,4},{6,5},{7,6},{8,15},{9,8},{10,9... | collective-permute-start | bytes 786440 | tf_op jit(solution)/shard_map/ppermute | solution.py:426
  21.2 19.3 %collective-permute-start.5 = (bf16[8,128,128]{2,1,0:T(8,128)(2,1)S(1)}, bf16[8,128,128]{2,1,0:T(8,128)(2,1)S(1)}, u32[]{:S(2)}, u32[]{:S(2)}) collective-permute-start(bf16[8,128,128]{2,1,0:T(8,128)(2,1)S(1)} %collective-permute-done.3.refs_4_), channel_id=1, source_target_pairs={{0,7},{1,0},{2,1},{3,2},{4,3},{5,4},{6,5},{7,6},{8,15},{9,8},{10,9... | collective-permute-start | bytes 786440 | tf_op jit(solution)/shard_map/ppermute | solution.py:426
  28.1 12.3 %collective-permute-start.6 = (bf16[8,128,128]{2,1,0:T(8,128)(2,1)S(1)}, bf16[8,128,128]{2,1,0:T(8,128)(2,1)S(1)}, u32[]{:S(2)}, u32[]{:S(2)}) collective-permute-start(bf16[8,128,128]{2,1,0:T(8,128)(2,1)S(1)} %collective-permute-done.4.refs_0_), channel_id=1, source_target_pairs={{0,1},{1,2},{2,3},{3,4},{4,5},{5,6},{6,7},{7,0},{8,9},{9,10},{10,1... | collective-permute-start | bytes 786440 | tf_op jit(solution)/shard_map/ppermute | solution.py:458
  29.5 11.0 %all-to-all-start = ((s32[8,1,8]{2,1,0:T(1,128)}), s32[8,1,8]{2,1,0:T(1,128)S(1)}, u32[]{:S(2)}, u32[]{:S(2)}) async-start(s32[8,1,8]{2,1,0:T(1,128)} %shard_map.104), calls=%async_computation | async-start | bytes 8192 | tf_op jit(solution)/shard_map/all_to_all | solution.py:501
  41.2 12.8 %collective-permute-start.7 = (bf16[12,128,128]{2,1,0:T(8,128)(2,1)S(1)}, bf16[12,128,128]{2,1,0:T(8,128)(2,1)S(1)}, u32[]{:S(2)}, u32[]{:S(2)}) collective-permute-start(bf16[12,128,128]{2,1,0:T(8,128)(2,1)S(1)} %get-tuple-element.19), channel_id=1, source_target_pairs={{0,8},{8,0},{16,24},{24,16},{32,40},{40,32},{48,56},{56,48},{1,9},... | collective-permute-start | bytes 1179656 | tf_op jit(solution)/shard_map/ppermute | solution.py:435
  49.4 30.7 %all-to-all-start.1 = ((bf16[8,5,128,128]{3,2,1,0:T(8,128)(2,1)}), bf16[8,5,128,128]{3,2,1,0:T(8,128)(2,1)S(1)}, u32[]{:S(2)}, u32[]{:S(2)}) async-start(bf16[8,5,128,128]{3,2,1,0:T(8,128)(2,1)} %shard_map.105), calls=%async_computation.1 | async-start | bytes 2621440 | tf_op jit(solution)/shard_map/all_to_all | solution.py:430
  54.1 20.4 %collective-permute-start.10 = (bf16[6,128,128]{2,1,0:T(8,128)(2,1)S(1)}, bf16[6,128,128]{2,1,0:T(8,128)(2,1)S(1)}, u32[]{:S(2)}, u32[]{:S(2)}) collective-permute-start(bf16[6,128,128]{2,1,0:T(8,128)(2,1)S(1)} %pad_maximum_fusion.3), channel_id=1, source_target_pairs={{0,48},{8,56},{16,0},{24,8},{32,16},{40,24},{48,32},{56,40},{1,49}... | collective-permute-start | bytes 589832 | tf_op jit(solution)/shard_map/ppermute | solution.py:441
  56.7 19.3 %collective-permute-start.9 = (bf16[6,128,128]{2,1,0:T(8,128)(2,1)S(1)}, bf16[6,128,128]{2,1,0:T(8,128)(2,1)S(1)}, u32[]{:S(2)}, u32[]{:S(2)}) collective-permute-start(bf16[6,128,128]{2,1,0:T(8,128)(2,1)S(1)} %pad_maximum_fusion.2), channel_id=1, source_target_pairs={{0,32},{8,40},{16,48},{24,56},{32,0},{40,8},{48,16},{56,24},{1,33}... | collective-permute-start | bytes 589832 | tf_op jit(solution)/shard_map/ppermute | solution.py:441
  57.4 22.7 %collective-permute-start.8 = (bf16[6,128,128]{2,1,0:T(8,128)(2,1)S(1)}, bf16[6,128,128]{2,1,0:T(8,128)(2,1)S(1)}, u32[]{:S(2)}, u32[]{:S(2)}) collective-permute-start(bf16[6,128,128]{2,1,0:T(8,128)(2,1)S(1)} %pad_maximum_fusion.1), channel_id=1, source_target_pairs={{0,16},{8,24},{16,32},{24,40},{32,48},{40,56},{48,0},{56,8},{1,17}... | collective-permute-start | bytes 589832 | tf_op jit(solution)/shard_map/ppermute | solution.py:441
  86.5 11.2 %collective-permute-start.12 = (bf16[7,128,128]{2,1,0:T(8,128)(2,1)S(1)}, bf16[7,128,128]{2,1,0:T(8,128)(2,1)S(1)}, u32[]{:S(2)}, u32[]{:S(2)}) collective-permute-start(bf16[7,128,128]{2,1,0:T(8,128)(2,1)S(1)} %shard_map.107.refs_0_), channel_id=1, source_target_pairs={{64,0},{128,64},{192,128},{0,192},{65,1},{129,65},{193,129},{1,193... | collective-permute-start | bytes 688136 | tf_op jit(solution)/shard_map/ppermute | solution.py:346
  87.9 9.7 %collective-permute-start.13 = (bf16[7,128,128]{2,1,0:T(8,128)(2,1)S(1)}, bf16[7,128,128]{2,1,0:T(8,128)(2,1)S(1)}, u32[]{:S(2)}, u32[]{:S(2)}) collective-permute-start(bf16[7,128,128]{2,1,0:T(8,128)(2,1)S(1)} %shard_map.107.refs_0_), channel_id=1, source_target_pairs={{0,8},{8,16},{16,24},{24,32},{32,40},{40,48},{48,56},{56,0},{1,9},... | collective-permute-start | bytes 688136 | tf_op jit(solution)/shard_map/ppermute | solution.py:345
  104.6 10.2 %collective-permute-start.17 = (f32[1,8,128]{2,1,0:T(8,128)S(1)}, f32[1,8,128]{2,1,0:T(8,128)S(1)}, u32[]{:S(2)}, u32[]{:S(2)}) collective-permute-start(f32[1,8,128]{2,1,0:T(8,128)S(1)} %get-tuple-element.41), channel_id=1, source_target_pairs={{64,0},{128,64},{192,128},{0,192},{65,1},{129,65},{193,129},{1,193... | collective-permute-start | bytes 12296 | tf_op jit(solution)/shard_map/ppermute | solution.py:359
  134.4 46.4 %all-to-all-start.2 = ((bf16[8,5,128,128]{3,2,1,0:T(8,128)(2,1)}), bf16[8,5,128,128]{3,2,1,0:T(8,128)(2,1)S(1)}, u32[]{:S(2)}, u32[]{:S(2)}) async-start(bf16[8,5,128,128]{3,2,1,0:T(8,128)(2,1)} %get-tuple-element.25), calls=%async_computation.2 | async-start | bytes 2621440 | tf_op jit(solution)/shard_map/all_to_all | solution.py:430
  143.7 16.7 %collective-permute-start.29 = (bf16[3,128,128]{2,1,0:T(8,128)(2,1)S(1)}, bf16[3,128,128]{2,1,0:T(8,128)(2,1)S(1)}, u32[]{:S(2)}, u32[]{:S(2)}) collective-permute-start(bf16[3,128,128]{2,1,0:T(8,128)(2,1)S(1)} %get-tuple-element.27), channel_id=1, source_target_pairs={{0,8},{8,16},{16,24},{24,32},{32,40},{40,48},{48,56},{56,0},{1,9},... | collective-permute-start | bytes 294920 | tf_op jit(solution)/shard_map/ppermute | solution.py:450
  145.3 20.0 %collective-permute-start.30 = (bf16[3,128,128]{2,1,0:T(8,128)(2,1)S(1)}, bf16[3,128,128]{2,1,0:T(8,128)(2,1)S(1)}, u32[]{:S(2)}, u32[]{:S(2)}) collective-permute-start(bf16[3,128,128]{2,1,0:T(8,128)(2,1)S(1)} %get-tuple-element.28), channel_id=1, source_target_pairs={{0,16},{8,24},{16,32},{24,40},{32,48},{40,56},{48,0},{56,8},{1,17}... | collective-permute-start | bytes 294920 | tf_op jit(solution)/shard_map/ppermute | solution.py:450
  146.5 19.7 %collective-permute-start.31 = (bf16[3,128,128]{2,1,0:T(8,128)(2,1)S(1)}, bf16[3,128,128]{2,1,0:T(8,128)(2,1)S(1)}, u32[]{:S(2)}, u32[]{:S(2)}) collective-permute-start(bf16[3,128,128]{2,1,0:T(8,128)(2,1)S(1)} %get-tuple-element.29), channel_id=1, source_target_pairs={{0,24},{8,32},{16,40},{24,48},{32,56},{40,0},{48,8},{56,16},{1,25}... | collective-permute-start | bytes 294920 | tf_op jit(solution)/shard_map/ppermute | solution.py:450
  148.1 21.5 %collective-permute-start.32 = (bf16[3,128,128]{2,1,0:T(8,128)(2,1)S(1)}, bf16[3,128,128]{2,1,0:T(8,128)(2,1)S(1)}, u32[]{:S(2)}, u32[]{:S(2)}) collective-permute-start(bf16[3,128,128]{2,1,0:T(8,128)(2,1)S(1)} %get-tuple-element.30), channel_id=1, source_target_pairs={{0,32},{8,40},{16,48},{24,56},{32,0},{40,8},{48,16},{56,24},{1,33}... | collective-permute-start | bytes 294920 | tf_op jit(solution)/shard_map/ppermute | solution.py:450
  148.7 21.5 %collective-permute-start.33 = (bf16[3,128,128]{2,1,0:T(8,128)(2,1)S(1)}, bf16[3,128,128]{2,1,0:T(8,128)(2,1)S(1)}, u32[]{:S(2)}, u32[]{:S(2)}) collective-permute-start(bf16[3,128,128]{2,1,0:T(8,128)(2,1)S(1)} %get-tuple-element.31), channel_id=1, source_target_pairs={{0,40},{8,48},{16,56},{24,0},{32,8},{40,16},{48,24},{56,32},{1,41}... | collective-permute-start | bytes 294920 | tf_op jit(solution)/shard_map/ppermute | solution.py:450
  160.4 9.8 %collective-permute-start.34 = (bf16[3,128,128]{2,1,0:T(8,128)(2,1)S(1)}, bf16[3,128,128]{2,1,0:T(8,128)(2,1)S(1)}, u32[]{:S(2)}, u32[]{:S(2)}) collective-permute-start(bf16[3,128,128]{2,1,0:T(8,128)(2,1)S(1)} %get-tuple-element.32), channel_id=1, source_target_pairs={{0,48},{8,56},{16,0},{24,8},{32,16},{40,24},{48,32},{56,40},{1,49}... | collective-permute-start | bytes 294920 | tf_op jit(solution)/shard_map/ppermute | solution.py:450
  171.0 9.0 %collective-permute-start.36 = (bf16[8,128,128]{2,1,0:T(8,128)(2,1)S(1)}, bf16[8,128,128]{2,1,0:T(8,128)(2,1)S(1)}, u32[]{:S(2)}, u32[]{:S(2)}) collective-permute-start(bf16[8,128,128]{2,1,0:T(8,128)(2,1)S(1)} %shard_map.112), channel_id=1, source_target_pairs={{0,1},{1,2},{2,3},{3,4},{4,5},{5,6},{6,7},{7,0},{8,9},{9,10},{10,1... | collective-permute-start | bytes 786440 | tf_op jit(solution)/shard_map/ppermute | solution.py:474
  171.9 8.9 %collective-permute-start.40 = (bf16[8,128,128]{2,1,0:T(8,128)(2,1)S(1)}, bf16[8,128,128]{2,1,0:T(8,128)(2,1)S(1)}, u32[]{:S(2)}, u32[]{:S(2)}) collective-permute-start(bf16[8,128,128]{2,1,0:T(8,128)(2,1)S(1)} %shard_map.116), channel_id=1, source_target_pairs={{0,7},{1,0},{2,1},{3,2},{4,3},{5,4},{6,5},{7,6},{8,15},{9,8},{10,9... | collective-permute-start | bytes 786440 | tf_op jit(solution)/shard_map/ppermute | solution.py:426
  180.7 8.8 %collective-permute-start.37 = (bf16[8,128,128]{2,1,0:T(8,128)(2,1)S(1)}, bf16[8,128,128]{2,1,0:T(8,128)(2,1)S(1)}, u32[]{:S(2)}, u32[]{:S(2)}) collective-permute-start(bf16[8,128,128]{2,1,0:T(8,128)(2,1)S(1)} %shard_map.113), channel_id=1, source_target_pairs={{0,1},{1,2},{2,3},{3,4},{4,5},{5,6},{6,7},{7,0},{8,9},{9,10},{10,1... | collective-permute-start | bytes 786440 | tf_op jit(solution)/shard_map/ppermute | solution.py:426
  181.7 8.8 %collective-permute-start.41 = (bf16[8,128,128]{2,1,0:T(8,128)(2,1)S(1)}, bf16[8,128,128]{2,1,0:T(8,128)(2,1)S(1)}, u32[]{:S(2)}, u32[]{:S(2)}) collective-permute-start(bf16[8,128,128]{2,1,0:T(8,128)(2,1)S(1)} %shard_map.117), channel_id=1, source_target_pairs={{0,7},{1,0},{2,1},{3,2},{4,3},{5,4},{6,5},{7,6},{8,15},{9,8},{10,9... | collective-permute-start | bytes 786440 | tf_op jit(solution)/shard_map/ppermute | solution.py:426
  (33 other events, 258.0 us)
where the time goes:
time: 208 us
  waiting for transfers between devices  96 us (46%)
  starting transfers between devices  75.2 us (36%)
  Pallas kernels  27.1 us (13%)
  local copies, waits for them, and re-layouts  7.62 us (4%)
    ppermute x12, waiting for transfers between devices, both_ways(): return (lax.ppermute(up, 'gz', ring(1)), lax.ppermute(down, 'gz', ring(-1)))  30.5 us
    pallas_call x15, Pallas kernels, call(): pl.pallas_call(kernel, out_shape=out_shape, in_specs=[SMEM] * smem + [VME...  25.7 us
    ppermute x3, waiting for transfers between devices, hand_over(): both = lax.ppermute(both, 'gy', pairs)  22 us
    ppermute x12, starting transfers between devices, both_ways(): return (lax.ppermute(up, 'gz', ring(1)), lax.ppermute(down, 'gz', ring(-1)))  21.2 us
    ppermute x7, waiting for transfers between devices, hand_back(): lax.ppermute(far[step], 'gy', [(i, (i + step) % size) for i in range(size)])  17.7 us
    all_to_all x2, starting transfers between devices, across(): return lax.all_to_all(x, 'gy', split_axis=0, concat_axis=0, tiled=True)  13.9 us
    ppermute x7, starting transfers between devices, hand_back(): lax.ppermute(far[step], 'gy', [(i, (i + step) % size) for i in range(size)])  8.83 us
    unnamed x22, local copies, waits for them, and re-layouts  7.34 us
  transfers between devices with their start and end apart: 46, of which 25 were waited for; matrix products, arithmetic and copies ran while one was open for 1% of the time, Pallas kernels for 4%

commit v1 on v0

--- a/solution.py
+++ b/solution.py
@@ -19,6 +19,8 @@
 HELD = 8
 NEAR = (0, -1, 1, -2, 2)
 FAR = (-3, 3, 4)
+EARLY = (0, 1, 2, 5, 6)
+LATE = (3, 4)
 SIDES = (("gx", 0), ("gy", 1), ("gz", 2))
 F32 = jnp.float32
 BF16 = jnp.bfloat16
@@ -119,13 +121,8 @@
                 total = total + 2.0 * jnp.sum((h * h).reshape(B // 8, 8, B), axis=0)
     norm = jnp.sum(jnp.sum(total, axis=0, keepdims=True), axis=1, keepdims=True)
     factor = lax.rsqrt(norm / M + EPSILON) / 1.3
-
-    def scaled(s, carry):
-        part = pl.ds(pl.multiple_of(s * B, B), B)
-        x_ref[part, :] = (h_ref[part, :] * factor).astype(BF16)
-        return carry
-
-    lax.fori_loop(0, S, scaled, 0)
+    for s in range(S):
+        x_ref[s * B : (s + 1) * B, :] = (h_ref[s * B : (s + 1) * B, :] * factor).astype(BF16)
     x0 = x_ref[...]
     for s in range(0, S, 2):
         part = slice(s * B, (s + 2) * B)
@@ -244,33 +241,47 @@
     lax.fori_loop(0, RMAX, slot, 0)
 
 
-def return_kernel(targets_ref, slots_ref, here_ref, *refs):
-    faces = refs[:7]
-    near_ref = refs[7]
-    far = refs[8 : 8 + N]
-    sum_ref = refs[8 + N]
+def add_grams(k, face_ref, targets_ref, slots_ref, here_ref, sum_ref):
+    def slot(r, carry):
+        target = targets_ref[k * RMAX + r]
+
+        @pl.when(target < S * S)
+        def _():
+            slot_id = slots_ref[target]
+            offset = wrapped(slot_id - here_ref[0])
+            at = offset * N + lax.div(slot_id, N)
+            total = sum_ref[at].astype(F32) + face_ref[r].astype(F32)
+            sum_ref[at] = total.astype(BF16)
+
+        return carry
+
+    lax.fori_loop(0, RMAX, slot, 0)
+
+
+def early_kernel(targets_ref, slots_ref, here_ref, *refs):
+    sum_ref = refs[-1]
 
     def clear(q, carry):
         sum_ref[q] = jnp.zeros((B, B), BF16)
         return carry
 
     lax.fori_loop(0, sum_ref.shape[0], clear, 0, unroll=8)
-    for k in range(7):
-
-        def slot(r, carry):
-            target = targets_ref[k * RMAX + r]
-
-            @pl.when(target < S * S)
-            def _():
-                slot_id = slots_ref[target]
-                offset = wrapped(slot_id - here_ref[0])
-                at = offset * N + lax.div(slot_id, N)
-                total = sum_ref[at].astype(F32) + faces[k][r].astype(F32)
-                sum_ref[at] = total.astype(BF16)
-
-            return carry
-
-        lax.fori_loop(0, RMAX, slot, 0)
+    for k, face_ref in zip(EARLY, refs):
+        add_grams(k, face_ref, targets_ref, slots_ref, here_ref, sum_ref)
+
+
+def return_kernel(targets_ref, slots_ref, here_ref, early_ref, *refs):
+    near_ref = refs[len(LATE)]
+    far = refs[len(LATE) + 1 : len(LATE) + 1 + N]
+    sum_ref = refs[-1]
+
+    def copied(q, carry):
+        sum_ref[q] = early_ref[q]
+        return carry
+
+    lax.fori_loop(0, sum_ref.shape[0], copied, 0, unroll=8)
+    for k, face_ref in zip(LATE, refs):
+        add_grams(k, face_ref, targets_ref, slots_ref, here_ref, sum_ref)
     for o, offset in enumerate(NEAR):
 
         def keep(i, carry):
@@ -307,34 +318,18 @@
             acc_ref[pick] = acc_ref[pick] + far[step][o].astype(F32)
 
 
-def farthest_kernel(table_ref, here_ref, *refs):
+def far_sums_kernel(chosen, table_ref, here_ref, *refs):
     far = refs[:N]
-    up_ref, acc_ref = refs[N:]
-    acc_ref[...] = jnp.zeros(acc_ref.shape, F32)
-    add_far(acc_ref, table_ref, here_ref, far, 2)
-    up_ref[...] = acc_ref[...].astype(BF16)
-
-
-def far_stage_kernel(o, table_ref, here_ref, *refs):
-    far = refs[:N]
-    next_ref, acc_ref = refs[-2:]
-    if len(refs) > N + 2:
-        acc_ref[...] = refs[N][...].astype(F32)
-    else:
-        acc_ref[...] = jnp.zeros(acc_ref.shape, F32)
-    add_far(acc_ref, table_ref, here_ref, far, o)
-    next_ref[...] = acc_ref[...].astype(BF16)
-
-
-def near_stage_kernel(o, table_ref, here_ref, near_ref, handed_ref, next_ref, acc_ref):
-    acc_ref[...] = handed_ref[...].astype(F32)
-    add_near(acc_ref, table_ref, wrapped(here_ref[0] + NEAR[o]), near_ref, o)
-    next_ref[...] = acc_ref[...].astype(BF16)
-
-
-def owner_kernel(table_ref, here_ref, near_ref, up_ref, down_ref, out_ref):
-    out_ref[...] = up_ref[...].astype(F32) + down_ref[...].astype(F32)
-    add_near(out_ref, table_ref, here_ref[0], near_ref, 0)
+    for k, o in enumerate(chosen):
+        out_ref = refs[N + k]
+        out_ref[...] = jnp.zeros(out_ref.shape, F32)
+        add_far(out_ref, table_ref, here_ref, far, o)
+
+
+def near_sums_kernel(chosen, table_ref, here_ref, near_ref, *outs):
+    for out_ref, o in zip(outs, chosen):
+        out_ref[...] = jnp.zeros(out_ref.shape, F32)
+        add_near(out_ref, table_ref, wrapped(here_ref[0] + NEAR[o]), near_ref, o)
 
 
 def face_exchange(x):
@@ -411,9 +406,12 @@
 
 
 def returned_of(targets, slots, here, grams):
+    tables = (targets, slots, here)
+    whole = shape((N * N, B, B), BF16)
+    early = call(early_kernel, whole, (*tables, *(grams[k] for k in EARLY)), 3)
     out = (shape((N, len(NEAR), B, B), BF16),) + (shape((len(FAR), B, B), BF16),) * N
-    ins = (targets, slots, here, *grams)
-    out = call(return_kernel, out, ins, 3, (pltpu.VMEM((N * N, B, B), BF16),))
+    ins = (*tables, early, *(grams[k] for k in LATE))
+    out = call(return_kernel, out, ins, 3, (pltpu.VMEM(whole.shape, BF16),))
     return out[0], out[1:]
 
 
@@ -466,24 +464,24 @@
 
 
 def brought_back(table, here, near, far):
-    acc = (pltpu.VMEM((HELD, B, B), F32),)
-    whole = shape((HELD, B, B), BF16)
+    def sums(kernel, chosen, parts):
+        out = (shape((HELD, B, B), F32),) * len(chosen)
+        return call(functools.partial(kernel, chosen), out, (table, here, *parts), 2)
+
     far = hand_back(far)
     near = across(near)
-    up = call(farthest_kernel, whole, (table, here, *far), 2, acc)
-    up = lax.ppermute(up, "gz", ring(1))
-    down = call(functools.partial(far_stage_kernel, 0), whole, (table, here, *far), 2, acc)
-    kernel = functools.partial(far_stage_kernel, 1)
-    up = call(kernel, whole, (table, here, *far, up), 2, acc)
-    for stage in (2, 1):
-        up, down = both_ways(up, down)
-        kernel = functools.partial(near_stage_kernel, 2 * stage)
-        up = call(kernel, whole, (table, here, near, up), 2, acc)
-        kernel = functools.partial(near_stage_kernel, 2 * stage - 1)
-        down = call(kernel, whole, (table, here, near, down), 2, acc)
-    up, down = both_ways(up, down)
-    ins = (table, here, near, up, down)
-    return call(owner_kernel, shape((HELD, B, B), F32), ins, 2)
+    (up,) = sums(far_sums_kernel, (2,), far)
+    up = lax.ppermute(up.astype(BF16), "gz", ring(1))
+    down3, up3 = sums(far_sums_kernel, (0, 1), far)
+    down = lax.ppermute(down3.astype(BF16), "gz", ring(-1))
+    up = lax.ppermute((up3 + up.astype(F32)).astype(BF16), "gz", ring(1))
+    down2, up2 = sums(near_sums_kernel, (3, 4), (near,))
+    down = lax.ppermute((down2 + down.astype(F32)).astype(BF16), "gz", ring(-1))
+    up = lax.ppermute((up2 + up.astype(F32)).astype(BF16), "gz", ring(1))
+    own, down1, up1 = sums(near_sums_kernel, (0, 1, 2), (near,))
+    down = lax.ppermute((down1 + down.astype(F32)).astype(BF16), "gz", ring(-1))
+    up = lax.ppermute((up1 + up.astype(F32)).astype(BF16), "gz", ring(1))
+    return own + down.astype(F32) + up.astype(F32)
 
 
 def shards(

time: 208 us -> 203 us (0.976)
  waiting for transfers between devices: 96 us -> 91.7 us
  Pallas kernels: 27.1 us -> 24 us
    ppermute x12 -> x6, waiting for transfers between devices: 30.5 us -> 15.6 us  [both_ways(): return (lax.ppermute(up, 'gz', ring(1)), lax.ppermute(down, 'gz', ring(-1)))]
    ppermute x1 -> x7, waiting for transfers between devices: 5.32 us -> 19.8 us  [the longest x1 6.32 us: brought_back(): up = lax.ppermute((up1 + up.astype(F32)).astype(BF16), 'gz', ring(1))]
    ppermute x12 -> x6, starting transfers between devices: 21.2 us -> 11.9 us  [both_ways(): return (lax.ppermute(up, 'gz', ring(1)), lax.ppermute(down, 'gz', ring(-1)))]
    ppermute x1 -> x7, starting transfers between devices: 0.08 us -> 9.05 us  [the longest x1 3.11 us: brought_back(): down = lax.ppermute((down2 + down.astype(F32)).astype(BF16), 'gz', ring(-1))]
    all_to_all x2, starting transfers between devices: 13.9 us -> 10.2 us  [across(): return lax.all_to_all(x, 'gy', split_axis=0, concat_axis=0, tiled=True)]
    ppermute x6, starting transfers between devices: 5.03 us -> 8.61 us  [face_exchange(): out.append(lax.ppermute(x, axis, [(b, a) for a, b in up]))]
    pallas_call x15 -> x12, Pallas kernels: 25.7 us -> 22.6 us  [call(): pl.pallas_call(kernel, out_shape=out_shape, in_specs=[SMEM] * smem + [VME...]
    ppermute x6, waiting for transfers between devices: 5.78 us -> 2.75 us  [face_exchange(): out.append(lax.ppermute(x, axis, up))]
  transfers between devices with their start and end apart: 46 -> 46, of which waited for: 25 -> 21; matrix products, arithmetic and copies ran while one was open for 1% -> 1% of each run, Pallas kernels for 4% -> 4%
where the time goes in v1:
time: 203 us; the launch traced here: 202 us
  waiting for transfers between devices  91.7 us (45%)
  starting transfers between devices  75.4 us (37%)
  Pallas kernels  24 us (12%)
  local copies, waits for them, and re-layouts  7.61 us (4%)
  other arithmetic  2.26 us (1%)
    pallas_call x12, Pallas kernels, call(): pl.pallas_call(kernel, out_shape=out_shape, in_specs=[SMEM] * smem + [VME...  22.6 us
    ppermute x3, waiting for transfers between devices, hand_over(): both = lax.ppermute(both, 'gy', pairs)  22 us
    ppermute x7, waiting for transfers between devices, hand_back(): lax.ppermute(far[step], 'gy', [(i, (i + step) % size) for i in range(size)])  17.7 us
    ppermute x6, waiting for transfers between devices, both_ways(): return (lax.ppermute(up, 'gz', ring(1)), lax.ppermute(down, 'gz', ring(-1)))  15.6 us
    ppermute x6, starting transfers between devices, both_ways(): return (lax.ppermute(up, 'gz', ring(1)), lax.ppermute(down, 'gz', ring(-1)))  11.9 us
    all_to_all x2, starting transfers between devices, across(): return lax.all_to_all(x, 'gy', split_axis=0, concat_axis=0, tiled=True)  10.2 us
    ppermute x7, starting transfers between devices, hand_back(): lax.ppermute(far[step], 'gy', [(i, (i + step) % size) for i in range(size)])  8.83 us
    ppermute x6, starting transfers between devices, face_exchange(): out.append(lax.ppermute(x, axis, [(b, a) for a, b in up]))  8.61 us
  transfers between devices with their start and end apart: 46, of which 21 were waited for; matrix products, arithmetic and copies ran while one was open for 1% of the time, Pallas kernels for 4%

profile of v1, /device:TPU:1, one launch (start us, length us, event | category | flops | bytes accessed | tf_op | source)
XLA Modules:
  0.0 202.0 jit_solution(16082215403979775178)
XLA Ops:
  3.2 4.0 %collective-permute-start.1 = (bf16[8,128,128]{2,1,0:T(8,128)(2,1)}, bf16[8,128,128]{2,1,0:T(8,128)(2,1)S(1)}, u32[]{:S(2)}, u32[]{:S(2)}) collective-permute-start(bf16[8,128,128]{2,1,0:T(8,128)(2,1)} %refs_0_.1), channel_id=1, source_target_pairs={{0,7},{1,0},{2,1},{3,2},{4,3},{5,4},{6,5},{7,6},{8,15},{9,8},{10,9... | collective-permute-start | bytes 786440 | tf_op jit(solution)/shard_map/ppermute | solution.py:424
  7.2 6.1 %collective-permute-done.refs_1_ = bf16[8,128,128]{2,1,0:T(8,128)(2,1)S(1)} collective-permute-done((bf16[8,128,128]{2,1,0:T(8,128)(2,1)}, bf16[8,128,128]{2,1,0:T(8,128)(2,1)S(1)}, u32[]{:S(2)}, u32[]{:S(2)}) %collective-permute-start) | collective-permute-done | bytes 262176 | tf_op jit(solution)/shard_map/ppermute | solution.py:424
  16.0 5.1 %collective-permute-done.2.refs_3_ = bf16[8,128,128]{2,1,0:T(8,128)(2,1)S(1)} collective-permute-done((bf16[8,128,128]{2,1,0:T(8,128)(2,1)S(1)}, bf16[8,128,128]{2,1,0:T(8,128)(2,1)S(1)}, u32[]{:S(2)}, u32[]{:S(2)}) %collective-permute-start.2) | collective-permute-done | bytes 262176 | tf_op jit(solution)/shard_map/ppermute | solution.py:424
  23.8 4.3 %collective-permute-done.4.refs_0_ = bf16[8,128,128]{2,1,0:T(8,128)(2,1)S(1)} collective-permute-done((bf16[8,128,128]{2,1,0:T(8,128)(2,1)S(1)}, bf16[8,128,128]{2,1,0:T(8,128)(2,1)S(1)}, u32[]{:S(2)}, u32[]{:S(2)}) %collective-permute-start.4) | collective-permute-done | bytes 262176 | tf_op jit(solution)/shard_map/ppermute | solution.py:424
  29.5 4.5 %all-to-all-start = ((s32[8,1,8]{2,1,0:T(1,128)}), s32[8,1,8]{2,1,0:T(1,128)S(1)}, u32[]{:S(2)}, u32[]{:S(2)}) async-start(s32[8,1,8]{2,1,0:T(1,128)} %shard_map.104), calls=%async_computation | async-start | bytes 8192 | tf_op jit(solution)/shard_map/all_to_all | solution.py:499
  34.1 6.4 %all-to-all-done.table_ref = s32[8,1,8]{2,1,0:T(1,128)S(1)} async-done(((s32[8,1,8]{2,1,0:T(1,128)}), s32[8,1,8]{2,1,0:T(1,128)S(1)}, u32[]{:S(2)}, u32[]{:S(2)}) %all-to-all-start) | async-done | bytes 288 | tf_op jit(solution)/shard_map/all_to_all | solution.py:499
  41.2 5.3 %collective-permute-start.7 = (bf16[12,128,128]{2,1,0:T(8,128)(2,1)S(1)}, bf16[12,128,128]{2,1,0:T(8,128)(2,1)S(1)}, u32[]{:S(2)}, u32[]{:S(2)}) collective-permute-start(bf16[12,128,128]{2,1,0:T(8,128)(2,1)S(1)} %get-tuple-element.26), channel_id=1, source_target_pairs={{0,8},{8,0},{16,24},{24,16},{32,40},{40,32},{48,56},{56,48},{1,9},... | collective-permute-start | bytes 1179656 | tf_op jit(solution)/shard_map/ppermute | solution.py:433
  49.4 4.6 %all-to-all-start.1 = ((bf16[8,5,128,128]{3,2,1,0:T(8,128)(2,1)}), bf16[8,5,128,128]{3,2,1,0:T(8,128)(2,1)S(1)}, u32[]{:S(2)}, u32[]{:S(2)}) async-start(bf16[8,5,128,128]{3,2,1,0:T(8,128)(2,1)} %shard_map.105), calls=%async_computation.1 | async-start | bytes 2621440 | tf_op jit(solution)/shard_map/all_to_all | solution.py:428
  58.1 16.4 %collective-permute-done.10.refs_4_ = bf16[6,128,128]{2,1,0:T(8,128)(2,1)S(1)} collective-permute-done((bf16[6,128,128]{2,1,0:T(8,128)(2,1)S(1)}, bf16[6,128,128]{2,1,0:T(8,128)(2,1)S(1)}, u32[]{:S(2)}, u32[]{:S(2)}) %collective-permute-start.10) | collective-permute-done | bytes 196640 | tf_op jit(solution)/shard_map/ppermute | solution.py:439
  76.0 4.1 %collective-permute-done.8.refs_2_ = bf16[6,128,128]{2,1,0:T(8,128)(2,1)S(1)} collective-permute-done((bf16[6,128,128]{2,1,0:T(8,128)(2,1)S(1)}, bf16[6,128,128]{2,1,0:T(8,128)(2,1)S(1)}, u32[]{:S(2)}, u32[]{:S(2)}) %collective-permute-start.8) | collective-permute-done | bytes 196640 | tf_op jit(solution)/shard_map/ppermute | solution.py:439
  80.1 4.6 %shard_map.107.refs_0_ = bf16[7,128,128]{2,1,0:T(8,128)(2,1)S(1)} custom-call(s32[36]{0:T(128)S(1)} %bitcast.25, s32[2]{0:T(128)S(1)} %pad_add_fusion.here_ref, bf16[8,5,128,128]{3,2,1,0:T(8,128)(2,1)S(1)} %all-to-all-done.1.refs_0_, bf16[6,128,128]{2,1,0:T(8,128)(2,1)S(1)} %pad_maximum_fusion.refs_1_, ...), custom_call_target="tpu_custom_call" | custom-call | tf_op jit(solution)/shard_map/pallas_call | solution.py:33
  100.2 4.1 %shard_map.109 = (f32[32,128]{1,0:T(8,128)S(1)}, f32[32,128]{1,0:T(8,128)S(1)}) custom-call(s32[8]{0:T(128)S(1)} %bitcast.28, s32[16]{0:T(128)S(1)} %reshape.30.pick_ref, bf16[7,128,128]{2,1,0:T(8,128)(2,1)S(1)} %shard_map.107.refs_0_, bf16[7,128,128]{2,1,0:T(8,128)(2,1)S(1)} %collective-permute-done.11.refs_1_, ...), custom_call_target="tpu_custom_call" | custom-call | tf_op jit(solution)/shard_map/pallas_call | solution.py:33
  105.8 3.1 %collective-permute-start.19 = (f32[4,1,128]{2,1,0:T(1,128)S(1)}, f32[4,1,128]{2,1,0:T(1,128)S(1)}, u32[]{:S(2)}, u32[]{:S(2)}) collective-permute-start(f32[4,1,128]{2,1,0:T(1,128)S(1)} %get-tuple-element.57), channel_id=1, source_target_pairs={{8,0},{16,8},{24,16},{32,24},{40,32},{48,40},{56,48},{0,56},{9,1},... | collective-permute-start | bytes 6152 | tf_op jit(solution)/shard_map/ppermute | solution.py:354
  114.6 3.4 %shard_map.110.refs_0_ = bf16[8,128,128]{2,1,0:T(8,128)(2,1)S(1)} custom-call(s32[16]{0:T(128)S(1)} %reshape.30.pick_ref, f32[32,128]{1,0:T(8,128)S(1)} %fusion.12.v_ref, bf16[512,4096]{1,0:T(8,128)(2,1)S(1)} %copy-done.2), custom_call_target="tpu_custom_call" | custom-call | tf_op jit(solution)/shard_map/pallas_call | solution.py:33
  123.4 3.0 %collective-permute-start.27 = (bf16[8,128,128]{2,1,0:T(8,128)(2,1)S(1)}, bf16[8,128,128]{2,1,0:T(8,128)(2,1)S(1)}, u32[]{:S(2)}, u32[]{:S(2)}) collective-permute-start(bf16[8,128,128]{2,1,0:T(8,128)(2,1)S(1)} %shard_map.110.refs_0_), channel_id=1, source_target_pairs={{0,8},{8,16},{16,24},{24,32},{32,40},{40,48},{48,56},{56,0},{1,9},... | collective-permute-start | bytes 786440 | tf_op jit(solution)/shard_map/ppermute | solution.py:340
  129.8 3.0 %collective-permute-done.28.refs_1_ = bf16[8,128,128]{2,1,0:T(8,128)(2,1)S(1)} collective-permute-done((bf16[8,128,128]{2,1,0:T(8,128)(2,1)S(1)}, bf16[8,128,128]{2,1,0:T(8,128)(2,1)S(1)}, u32[]{:S(2)}, u32[]{:S(2)}) %collective-permute-start.28) | collective-permute-done | bytes 262176 | tf_op jit(solution)/shard_map/ppermute | solution.py:341
  135.0 5.6 %all-to-all-start.2 = ((bf16[8,5,128,128]{3,2,1,0:T(8,128)(2,1)}), bf16[8,5,128,128]{3,2,1,0:T(8,128)(2,1)S(1)}, u32[]{:S(2)}, u32[]{:S(2)}) async-start(bf16[8,5,128,128]{3,2,1,0:T(8,128)(2,1)} %get-tuple-element.32), calls=%async_computation.2 | async-start | bytes 2621440 | tf_op jit(solution)/shard_map/all_to_all | solution.py:428
  147.3 10.1 %collective-permute-done.29.refs_1_ = bf16[3,128,128]{2,1,0:T(8,128)(2,1)S(1)} collective-permute-done((bf16[3,128,128]{2,1,0:T(8,128)(2,1)S(1)}, bf16[3,128,128]{2,1,0:T(8,128)(2,1)S(1)}, u32[]{:S(2)}, u32[]{:S(2)}) %collective-permute-start.29) | collective-permute-done | bytes 98336 | tf_op jit(solution)/shard_map/ppermute | solution.py:448
  163.2 3.5 %collective-permute-done.32.refs_4_ = bf16[3,128,128]{2,1,0:T(8,128)(2,1)S(1)} collective-permute-done((bf16[3,128,128]{2,1,0:T(8,128)(2,1)S(1)}, bf16[3,128,128]{2,1,0:T(8,128)(2,1)S(1)}, u32[]{:S(2)}, u32[]{:S(2)}) %collective-permute-start.32) | collective-permute-done | bytes 98336 | tf_op jit(solution)/shard_map/ppermute | solution.py:448
  171.8 5.1 %collective-permute-done.39 = bf16[8,128,128]{2,1,0:T(8,128)(2,1)S(1)} collective-permute-done((bf16[8,128,128]{2,1,0:T(8,128)(2,1)S(1)}, bf16[8,128,128]{2,1,0:T(8,128)(2,1)S(1)}, u32[]{:S(2)}, u32[]{:S(2)}) %collective-permute-start.39) | collective-permute-done | bytes 262176 | tf_op jit(solution)/shard_map/ppermute | solution.py:474
  178.2 3.1 %collective-permute-start.37 = (bf16[8,128,128]{2,1,0:T(8,128)(2,1)S(1)}, bf16[8,128,128]{2,1,0:T(8,128)(2,1)S(1)}, u32[]{:S(2)}, u32[]{:S(2)}) collective-permute-start(bf16[8,128,128]{2,1,0:T(8,128)(2,1)S(1)} %add_convert_fusion.4), channel_id=1, source_target_pairs={{0,7},{1,0},{2,1},{3,2},{4,3},{5,4},{6,5},{7,6},{8,15},{9,8},{10,9... | collective-permute-start | bytes 786440 | tf_op jit(solution)/shard_map/ppermute | solution.py:479
  181.3 4.6 %collective-permute-done.40 = bf16[8,128,128]{2,1,0:T(8,128)(2,1)S(1)} collective-permute-done((bf16[8,128,128]{2,1,0:T(8,128)(2,1)S(1)}, bf16[8,128,128]{2,1,0:T(8,128)(2,1)S(1)}, u32[]{:S(2)}, u32[]{:S(2)}) %collective-permute-start.40) | collective-permute-done | bytes 262176 | tf_op jit(solution)/shard_map/ppermute | solution.py:477
  190.1 3.8 %collective-permute-done.41 = bf16[8,128,128]{2,1,0:T(8,128)(2,1)S(1)} collective-permute-done((bf16[8,128,128]{2,1,0:T(8,128)(2,1)S(1)}, bf16[8,128,128]{2,1,0:T(8,128)(2,1)S(1)}, u32[]{:S(2)}, u32[]{:S(2)}) %collective-permute-start.41) | collective-permute-done | bytes 262176 | tf_op jit(solution)/shard_map/ppermute | solution.py:480
  194.8 6.3 %collective-permute-done.42 = bf16[8,128,128]{2,1,0:T(8,128)(2,1)S(1)} collective-permute-done((bf16[8,128,128]{2,1,0:T(8,128)(2,1)S(1)}, bf16[8,128,128]{2,1,0:T(8,128)(2,1)S(1)}, u32[]{:S(2)}, u32[]{:S(2)}) %collective-permute-start.42) | collective-permute-done | bytes 262176 | tf_op jit(solution)/shard_map/ppermute | solution.py:483
  (127 shorter events, 76.9 us)
Async XLA Ops:
  0.6 12.7 %collective-permute-start = (bf16[8,128,128]{2,1,0:T(8,128)(2,1)}, bf16[8,128,128]{2,1,0:T(8,128)(2,1)S(1)}, u32[]{:S(2)}, u32[]{:S(2)}) collective-permute-start(bf16[8,128,128]{2,1,0:T(8,128)(2,1)} %refs_0_.1), channel_id=1, source_target_pairs={{0,1},{1,2},{2,3},{3,4},{4,5},{5,6},{6,7},{7,0},{8,9},{9,10},{10,1... | collective-permute-start | bytes 786440 | tf_op jit(solution)/shard_map/ppermute | solution.py:424
  3.2 10.2 %collective-permute-start.1 = (bf16[8,128,128]{2,1,0:T(8,128)(2,1)}, bf16[8,128,128]{2,1,0:T(8,128)(2,1)S(1)}, u32[]{:S(2)}, u32[]{:S(2)}) collective-permute-start(bf16[8,128,128]{2,1,0:T(8,128)(2,1)} %refs_0_.1), channel_id=1, source_target_pairs={{0,7},{1,0},{2,1},{3,2},{4,3},{5,4},{6,5},{7,6},{8,15},{9,8},{10,9... | collective-permute-start | bytes 786440 | tf_op jit(solution)/shard_map/ppermute | solution.py:424
  21.2 19.3 %collective-permute-start.5 = (bf16[8,128,128]{2,1,0:T(8,128)(2,1)S(1)}, bf16[8,128,128]{2,1,0:T(8,128)(2,1)S(1)}, u32[]{:S(2)}, u32[]{:S(2)}) collective-permute-start(bf16[8,128,128]{2,1,0:T(8,128)(2,1)S(1)} %collective-permute-done.3.refs_4_), channel_id=1, source_target_pairs={{0,7},{1,0},{2,1},{3,2},{4,3},{5,4},{6,5},{7,6},{8,15},{9,8},{10,9... | collective-permute-start | bytes 786440 | tf_op jit(solution)/shard_map/ppermute | solution.py:424
  28.1 12.3 %collective-permute-start.6 = (bf16[8,128,128]{2,1,0:T(8,128)(2,1)S(1)}, bf16[8,128,128]{2,1,0:T(8,128)(2,1)S(1)}, u32[]{:S(2)}, u32[]{:S(2)}) collective-permute-start(bf16[8,128,128]{2,1,0:T(8,128)(2,1)S(1)} %collective-permute-done.4.refs_0_), channel_id=1, source_target_pairs={{0,1},{1,2},{2,3},{3,4},{4,5},{5,6},{6,7},{7,0},{8,9},{9,10},{10,1... | collective-permute-start | bytes 786440 | tf_op jit(solution)/shard_map/ppermute | solution.py:456
  29.5 11.0 %all-to-all-start = ((s32[8,1,8]{2,1,0:T(1,128)}), s32[8,1,8]{2,1,0:T(1,128)S(1)}, u32[]{:S(2)}, u32[]{:S(2)}) async-start(s32[8,1,8]{2,1,0:T(1,128)} %shard_map.104), calls=%async_computation | async-start | bytes 8192 | tf_op jit(solution)/shard_map/all_to_all | solution.py:499
  41.2 12.8 %collective-permute-start.7 = (bf16[12,128,128]{2,1,0:T(8,128)(2,1)S(1)}, bf16[12,128,128]{2,1,0:T(8,128)(2,1)S(1)}, u32[]{:S(2)}, u32[]{:S(2)}) collective-permute-start(bf16[12,128,128]{2,1,0:T(8,128)(2,1)S(1)} %get-tuple-element.26), channel_id=1, source_target_pairs={{0,8},{8,0},{16,24},{24,16},{32,40},{40,32},{48,56},{56,48},{1,9},... | collective-permute-start | bytes 1179656 | tf_op jit(solution)/shard_map/ppermute | solution.py:433
  49.4 30.7 %all-to-all-start.1 = ((bf16[8,5,128,128]{3,2,1,0:T(8,128)(2,1)}), bf16[8,5,128,128]{3,2,1,0:T(8,128)(2,1)S(1)}, u32[]{:S(2)}, u32[]{:S(2)}) async-start(bf16[8,5,128,128]{3,2,1,0:T(8,128)(2,1)} %shard_map.105), calls=%async_computation.1 | async-start | bytes 2621440 | tf_op jit(solution)/shard_map/all_to_all | solution.py:428
  54.1 20.4 %collective-permute-start.10 = (bf16[6,128,128]{2,1,0:T(8,128)(2,1)S(1)}, bf16[6,128,128]{2,1,0:T(8,128)(2,1)S(1)}, u32[]{:S(2)}, u32[]{:S(2)}) collective-permute-start(bf16[6,128,128]{2,1,0:T(8,128)(2,1)S(1)} %pad_maximum_fusion.3), channel_id=1, source_target_pairs={{0,48},{8,56},{16,0},{24,8},{32,16},{40,24},{48,32},{56,40},{1,49}... | collective-permute-start | bytes 589832 | tf_op jit(solution)/shard_map/ppermute | solution.py:439
  56.7 19.3 %collective-permute-start.9 = (bf16[6,128,128]{2,1,0:T(8,128)(2,1)S(1)}, bf16[6,128,128]{2,1,0:T(8,128)(2,1)S(1)}, u32[]{:S(2)}, u32[]{:S(2)}) collective-permute-start(bf16[6,128,128]{2,1,0:T(8,128)(2,1)S(1)} %pad_maximum_fusion.2), channel_id=1, source_target_pairs={{0,32},{8,40},{16,48},{24,56},{32,0},{40,8},{48,16},{56,24},{1,33}... | collective-permute-start | bytes 589832 | tf_op jit(solution)/shard_map/ppermute | solution.py:439
  57.4 22.7 %collective-permute-start.8 = (bf16[6,128,128]{2,1,0:T(8,128)(2,1)S(1)}, bf16[6,128,128]{2,1,0:T(8,128)(2,1)S(1)}, u32[]{:S(2)}, u32[]{:S(2)}) collective-permute-start(bf16[6,128,128]{2,1,0:T(8,128)(2,1)S(1)} %pad_maximum_fusion.1), channel_id=1, source_target_pairs={{0,16},{8,24},{16,32},{24,40},{32,48},{40,56},{48,0},{56,8},{1,17}... | collective-permute-start | bytes 589832 | tf_op jit(solution)/shard_map/ppermute | solution.py:439
  86.1 11.2 %collective-permute-start.12 = (bf16[7,128,128]{2,1,0:T(8,128)(2,1)S(1)}, bf16[7,128,128]{2,1,0:T(8,128)(2,1)S(1)}, u32[]{:S(2)}, u32[]{:S(2)}) collective-permute-start(bf16[7,128,128]{2,1,0:T(8,128)(2,1)S(1)} %shard_map.107.refs_0_), channel_id=1, source_target_pairs={{64,0},{128,64},{192,128},{0,192},{65,1},{129,65},{193,129},{1,193... | collective-permute-start | bytes 688136 | tf_op jit(solution)/shard_map/ppermute | solution.py:341
  87.6 9.7 %collective-permute-start.13 = (bf16[7,128,128]{2,1,0:T(8,128)(2,1)S(1)}, bf16[7,128,128]{2,1,0:T(8,128)(2,1)S(1)}, u32[]{:S(2)}, u32[]{:S(2)}) collective-permute-start(bf16[7,128,128]{2,1,0:T(8,128)(2,1)S(1)} %shard_map.107.refs_0_), channel_id=1, source_target_pairs={{0,8},{8,16},{16,24},{24,32},{32,40},{40,48},{48,56},{56,0},{1,9},... | collective-permute-start | bytes 688136 | tf_op jit(solution)/shard_map/ppermute | solution.py:340
  104.3 10.2 %collective-permute-start.17 = (f32[1,8,128]{2,1,0:T(8,128)S(1)}, f32[1,8,128]{2,1,0:T(8,128)S(1)}, u32[]{:S(2)}, u32[]{:S(2)}) collective-permute-start(f32[1,8,128]{2,1,0:T(8,128)S(1)} %get-tuple-element.55), channel_id=1, source_target_pairs={{64,0},{128,64},{192,128},{0,192},{65,1},{129,65},{193,129},{1,193... | collective-permute-start | bytes 12296 | tf_op jit(solution)/shard_map/ppermute | solution.py:354
  118.1 10.0 %collective-permute-start.24 = (bf16[8,128,128]{2,1,0:T(8,128)(2,1)S(1)}, bf16[8,128,128]{2,1,0:T(8,128)(2,1)S(1)}, u32[]{:S(2)}, u32[]{:S(2)}) collective-permute-start(bf16[8,128,128]{2,1,0:T(8,128)(2,1)S(1)} %shard_map.110.refs_0_), channel_id=1, source_target_pairs={{64,0},{128,64},{192,128},{0,192},{65,1},{129,65},{193,129},{1,193... | collective-permute-start | bytes 786440 | tf_op jit(solution)/shard_map/ppermute | solution.py:341
  135.0 42.1 %all-to-all-start.2 = ((bf16[8,5,128,128]{3,2,1,0:T(8,128)(2,1)}), bf16[8,5,128,128]{3,2,1,0:T(8,128)(2,1)S(1)}, u32[]{:S(2)}, u32[]{:S(2)}) async-start(bf16[8,5,128,128]{3,2,1,0:T(8,128)(2,1)} %get-tuple-element.32), calls=%async_computation.2 | async-start | bytes 2621440 | tf_op jit(solution)/shard_map/all_to_all | solution.py:428
  140.7 16.7 %collective-permute-start.29 = (bf16[3,128,128]{2,1,0:T(8,128)(2,1)S(1)}, bf16[3,128,128]{2,1,0:T(8,128)(2,1)S(1)}, u32[]{:S(2)}, u32[]{:S(2)}) collective-permute-start(bf16[3,128,128]{2,1,0:T(8,128)(2,1)S(1)} %get-tuple-element.37), channel_id=1, source_target_pairs={{0,8},{8,16},{16,24},{24,32},{32,40},{40,48},{48,56},{56,0},{1,9},... | collective-permute-start | bytes 294920 | tf_op jit(solution)/shard_map/ppermute | solution.py:448
  142.3 20.0 %collective-permute-start.30 = (bf16[3,128,128]{2,1,0:T(8,128)(2,1)S(1)}, bf16[3,128,128]{2,1,0:T(8,128)(2,1)S(1)}, u32[]{:S(2)}, u32[]{:S(2)}) collective-permute-start(bf16[3,128,128]{2,1,0:T(8,128)(2,1)S(1)} %get-tuple-element.38), channel_id=1, source_target_pairs={{0,16},{8,24},{16,32},{24,40},{32,48},{40,56},{48,0},{56,8},{1,17}... | collective-permute-start | bytes 294920 | tf_op jit(solution)/shard_map/ppermute | solution.py:448
  143.5 19.7 %collective-permute-start.31 = (bf16[3,128,128]{2,1,0:T(8,128)(2,1)S(1)}, bf16[3,128,128]{2,1,0:T(8,128)(2,1)S(1)}, u32[]{:S(2)}, u32[]{:S(2)}) collective-permute-start(bf16[3,128,128]{2,1,0:T(8,128)(2,1)S(1)} %get-tuple-element.39), channel_id=1, source_target_pairs={{0,24},{8,32},{16,40},{24,48},{32,56},{40,0},{48,8},{56,16},{1,25}... | collective-permute-start | bytes 294920 | tf_op jit(solution)/shard_map/ppermute | solution.py:448
  145.1 21.5 %collective-permute-start.32 = (bf16[3,128,128]{2,1,0:T(8,128)(2,1)S(1)}, bf16[3,128,128]{2,1,0:T(8,128)(2,1)S(1)}, u32[]{:S(2)}, u32[]{:S(2)}) collective-permute-start(bf16[3,128,128]{2,1,0:T(8,128)(2,1)S(1)} %get-tuple-element.40), channel_id=1, source_target_pairs={{0,32},{8,40},{16,48},{24,56},{32,0},{40,8},{48,16},{56,24},{1,33}... | collective-permute-start | bytes 294920 | tf_op jit(solution)/shard_map/ppermute | solution.py:448
  145.7 21.5 %collective-permute-start.33 = (bf16[3,128,128]{2,1,0:T(8,128)(2,1)S(1)}, bf16[3,128,128]{2,1,0:T(8,128)(2,1)S(1)}, u32[]{:S(2)}, u32[]{:S(2)}) collective-permute-start(bf16[3,128,128]{2,1,0:T(8,128)(2,1)S(1)} %get-tuple-element.41), channel_id=1, source_target_pairs={{0,40},{8,48},{16,56},{24,0},{32,8},{40,16},{48,24},{56,32},{1,41}... | collective-permute-start | bytes 294920 | tf_op jit(solution)/shard_map/ppermute | solution.py:448
  157.4 9.8 %collective-permute-start.34 = (bf16[3,128,128]{2,1,0:T(8,128)(2,1)S(1)}, bf16[3,128,128]{2,1,0:T(8,128)(2,1)S(1)}, u32[]{:S(2)}, u32[]{:S(2)}) collective-permute-start(bf16[3,128,128]{2,1,0:T(8,128)(2,1)S(1)} %get-tuple-element.42), channel_id=1, source_target_pairs={{0,48},{8,56},{16,0},{24,8},{32,16},{40,24},{48,32},{56,40},{1,49}... | collective-permute-start | bytes 294920 | tf_op jit(solution)/shard_map/ppermute | solution.py:448
  168.0 9.0 %collective-permute-start.39 = (bf16[8,128,128]{2,1,0:T(8,128)(2,1)S(1)}, bf16[8,128,128]{2,1,0:T(8,128)(2,1)S(1)}, u32[]{:S(2)}, u32[]{:S(2)}) collective-permute-start(bf16[8,128,128]{2,1,0:T(8,128)(2,1)S(1)} %convert_element_type.54), channel_id=1, source_target_pairs={{0,1},{1,2},{2,3},{3,4},{4,5},{5,6},{6,7},{7,0},{8,9},{9,10},{10,1... | collective-permute-start | bytes 786440 | tf_op jit(solution)/shard_map/ppermute | solution.py:474
  169.1 9.1 %collective-permute-start.36 = (bf16[8,128,128]{2,1,0:T(8,128)(2,1)S(1)}, bf16[8,128,128]{2,1,0:T(8,128)(2,1)S(1)}, u32[]{:S(2)}, u32[]{:S(2)}) collective-permute-start(bf16[8,128,128]{2,1,0:T(8,128)(2,1)S(1)} %convert_element_type.48), channel_id=1, source_target_pairs={{0,7},{1,0},{2,1},{3,2},{4,3},{5,4},{6,5},{7,6},{8,15},{9,8},{10,9... | collective-permute-start | bytes 786440 | tf_op jit(solution)/shard_map/ppermute | solution.py:476
  178.2 9.0 %collective-permute-start.37 = (bf16[8,128,128]{2,1,0:T(8,128)(2,1)S(1)}, bf16[8,128,128]{2,1,0:T(8,128)(2,1)S(1)}, u32[]{:S(2)}, u32[]{:S(2)}) collective-permute-start(bf16[8,128,128]{2,1,0:T(8,128)(2,1)S(1)} %add_convert_fusion.4), channel_id=1, source_target_pairs={{0,7},{1,0},{2,1},{3,2},{4,3},{5,4},{6,5},{7,6},{8,15},{9,8},{10,9... | collective-permute-start | bytes 786440 | tf_op jit(solution)/shard_map/ppermute | solution.py:479
  (33 other events, 264.4 us)

commit v2 on v1

--- a/solution.py
+++ b/solution.py
@@ -145,8 +145,15 @@
         out_ref[s] = (0.5 * value).astype(BF16)
 
 
-def hold_kernel(phi_ref, out_ref):
-    out_ref[...] = phi_ref[...]
+def hold_kernel(in_ref, out_ref):
+    size = in_ref.shape[0] // 8
+
+    def some(i, carry):
+        part = pl.ds(pl.multiple_of(i * size, size), size)
+        out_ref[part] = in_ref[part]
+        return carry
+
+    lax.fori_loop(0, 8, some, 0)
 
 
 def turn_kernel(picks_ref, out_ref):
@@ -454,7 +461,8 @@
     up2, down2 = both_ways(up1, down1)
     up3, down3 = both_ways(up2, down2)
     up4 = lax.ppermute(up3, "gz", ring(1))
-    ins = (table, here, ham_blocks, up1, down1, up2, down2)
+    own = call(hold_kernel, shape(ham_blocks.shape, BF16), (ham_blocks,), 0)
+    ins = (table, here, own, up1, down1, up2, down2)
     near = call(near_kernel, shape((N, len(NEAR), B, B), BF16), ins, 2)
     near = across(near)
     ins = (table, here, up3, down3, up4)

time: 203 us -> 203 us (level)
    pallas_call x12 -> x13, Pallas kernels: 22.6 us -> 22.7 us  [call(): pl.pallas_call(kernel, out_shape=out_shape, in_specs=[SMEM] * smem + [VME...]
  transfers between devices with their start and end apart: 46 -> 46, of which waited for: 21 -> 21; matrix products, arithmetic and copies ran while one was open for 1% -> 1% of each run, Pallas kernels for 4% -> 5%
where the time goes in v2:
time: 203 us; the launch traced here: 202 us
  waiting for transfers between devices  91.7 us (45%)
  starting transfers between devices  75.4 us (37%)
  Pallas kernels  24.1 us (12%)
  local copies, waits for them, and re-layouts  7.61 us (4%)
  other arithmetic  2.25 us (1%)
    pallas_call x13, Pallas kernels, call(): pl.pallas_call(kernel, out_shape=out_shape, in_specs=[SMEM] * smem + [VME...  22.7 us
    ppermute x3, waiting for transfers between devices, hand_over(): both = lax.ppermute(both, 'gy', pairs)  22 us
    ppermute x7, waiting for transfers between devices, hand_back(): lax.ppermute(far[step], 'gy', [(i, (i + step) % size) for i in range(size)])  17.7 us
    ppermute x6, waiting for transfers between devices, both_ways(): return (lax.ppermute(up, 'gz', ring(1)), lax.ppermute(down, 'gz', ring(-1)))  15.6 us
    ppermute x6, starting transfers between devices, both_ways(): return (lax.ppermute(up, 'gz', ring(1)), lax.ppermute(down, 'gz', ring(-1)))  11.9 us
    all_to_all x2, starting transfers between devices, across(): return lax.all_to_all(x, 'gy', split_axis=0, concat_axis=0, tiled=True)  10.2 us
    ppermute x7, starting transfers between devices, hand_back(): lax.ppermute(far[step], 'gy', [(i, (i + step) % size) for i in range(size)])  8.83 us
    ppermute x6, starting transfers between devices, face_exchange(): out.append(lax.ppermute(x, axis, [(b, a) for a, b in up]))  8.61 us
  transfers between devices with their start and end apart: 46, of which 21 were waited for; matrix products, arithmetic and copies ran while one was open for 1% of the time, Pallas kernels for 5%

profile of v2, /device:TPU:1, one launch (start us, length us, event | category | flops | bytes accessed | tf_op | source)
XLA Modules:
  0.0 202.1 jit_solution(13154853606585818744)
XLA Ops:
  3.2 4.0 %collective-permute-start.1 = (bf16[8,128,128]{2,1,0:T(8,128)(2,1)}, bf16[8,128,128]{2,1,0:T(8,128)(2,1)S(1)}, u32[]{:S(2)}, u32[]{:S(2)}) collective-permute-start(bf16[8,128,128]{2,1,0:T(8,128)(2,1)} %in_ref.1), channel_id=1, source_target_pairs={{0,7},{1,0},{2,1},{3,2},{4,3},{5,4},{6,5},{7,6},{8,15},{9,8},{10,9... | collective-permute-start | bytes 786440 | tf_op jit(solution)/shard_map/ppermute | solution.py:431
  7.2 6.1 %collective-permute-done.refs_1_ = bf16[8,128,128]{2,1,0:T(8,128)(2,1)S(1)} collective-permute-done((bf16[8,128,128]{2,1,0:T(8,128)(2,1)}, bf16[8,128,128]{2,1,0:T(8,128)(2,1)S(1)}, u32[]{:S(2)}, u32[]{:S(2)}) %collective-permute-start) | collective-permute-done | bytes 262176 | tf_op jit(solution)/shard_map/ppermute | solution.py:431
  16.0 5.1 %collective-permute-done.2.refs_3_ = bf16[8,128,128]{2,1,0:T(8,128)(2,1)S(1)} collective-permute-done((bf16[8,128,128]{2,1,0:T(8,128)(2,1)S(1)}, bf16[8,128,128]{2,1,0:T(8,128)(2,1)S(1)}, u32[]{:S(2)}, u32[]{:S(2)}) %collective-permute-start.2) | collective-permute-done | bytes 262176 | tf_op jit(solution)/shard_map/ppermute | solution.py:431
  23.8 4.3 %collective-permute-done.4.refs_0_ = bf16[8,128,128]{2,1,0:T(8,128)(2,1)S(1)} collective-permute-done((bf16[8,128,128]{2,1,0:T(8,128)(2,1)S(1)}, bf16[8,128,128]{2,1,0:T(8,128)(2,1)S(1)}, u32[]{:S(2)}, u32[]{:S(2)}) %collective-permute-start.4) | collective-permute-done | bytes 262176 | tf_op jit(solution)/shard_map/ppermute | solution.py:431
  29.5 4.5 %all-to-all-start = ((s32[8,1,8]{2,1,0:T(1,128)}), s32[8,1,8]{2,1,0:T(1,128)S(1)}, u32[]{:S(2)}, u32[]{:S(2)}) async-start(s32[8,1,8]{2,1,0:T(1,128)} %shard_map.104), calls=%async_computation | async-start | bytes 8192 | tf_op jit(solution)/shard_map/all_to_all | solution.py:507
  34.1 6.4 %all-to-all-done.table_ref = s32[8,1,8]{2,1,0:T(1,128)S(1)} async-done(((s32[8,1,8]{2,1,0:T(1,128)}), s32[8,1,8]{2,1,0:T(1,128)S(1)}, u32[]{:S(2)}, u32[]{:S(2)}) %all-to-all-start) | async-done | bytes 288 | tf_op jit(solution)/shard_map/all_to_all | solution.py:507
  41.2 5.3 %collective-permute-start.7 = (bf16[12,128,128]{2,1,0:T(8,128)(2,1)S(1)}, bf16[12,128,128]{2,1,0:T(8,128)(2,1)S(1)}, u32[]{:S(2)}, u32[]{:S(2)}) collective-permute-start(bf16[12,128,128]{2,1,0:T(8,128)(2,1)S(1)} %get-tuple-element.26), channel_id=1, source_target_pairs={{0,8},{8,0},{16,24},{24,16},{32,40},{40,32},{48,56},{56,48},{1,9},... | collective-permute-start | bytes 1179656 | tf_op jit(solution)/shard_map/ppermute | solution.py:440
  49.4 4.6 %all-to-all-start.1 = ((bf16[8,5,128,128]{3,2,1,0:T(8,128)(2,1)}), bf16[8,5,128,128]{3,2,1,0:T(8,128)(2,1)S(1)}, u32[]{:S(2)}, u32[]{:S(2)}) async-start(bf16[8,5,128,128]{3,2,1,0:T(8,128)(2,1)} %shard_map.106), calls=%async_computation.1 | async-start | bytes 2621440 | tf_op jit(solution)/shard_map/all_to_all | solution.py:435
  58.1 16.4 %collective-permute-done.10.refs_4_ = bf16[6,128,128]{2,1,0:T(8,128)(2,1)S(1)} collective-permute-done((bf16[6,128,128]{2,1,0:T(8,128)(2,1)S(1)}, bf16[6,128,128]{2,1,0:T(8,128)(2,1)S(1)}, u32[]{:S(2)}, u32[]{:S(2)}) %collective-permute-start.10) | collective-permute-done | bytes 196640 | tf_op jit(solution)/shard_map/ppermute | solution.py:446
  76.1 4.1 %collective-permute-done.8.refs_2_ = bf16[6,128,128]{2,1,0:T(8,128)(2,1)S(1)} collective-permute-done((bf16[6,128,128]{2,1,0:T(8,128)(2,1)S(1)}, bf16[6,128,128]{2,1,0:T(8,128)(2,1)S(1)}, u32[]{:S(2)}, u32[]{:S(2)}) %collective-permute-start.8) | collective-permute-done | bytes 196640 | tf_op jit(solution)/shard_map/ppermute | solution.py:446
  80.1 4.6 %shard_map.108.refs_0_ = bf16[7,128,128]{2,1,0:T(8,128)(2,1)S(1)} custom-call(s32[36]{0:T(128)S(1)} %bitcast.25, s32[2]{0:T(128)S(1)} %pad_add_fusion.here_ref, bf16[8,5,128,128]{3,2,1,0:T(8,128)(2,1)S(1)} %all-to-all-done.1.refs_0_, bf16[6,128,128]{2,1,0:T(8,128)(2,1)S(1)} %pad_maximum_fusion.refs_1_, ...), custom_call_target="tpu_custom_call" | custom-call | tf_op jit(solution)/shard_map/pallas_call | solution.py:33
  100.2 4.1 %shard_map.110 = (f32[32,128]{1,0:T(8,128)S(1)}, f32[32,128]{1,0:T(8,128)S(1)}) custom-call(s32[8]{0:T(128)S(1)} %bitcast.28, s32[16]{0:T(128)S(1)} %reshape.30.pick_ref, bf16[7,128,128]{2,1,0:T(8,128)(2,1)S(1)} %shard_map.108.refs_0_, bf16[7,128,128]{2,1,0:T(8,128)(2,1)S(1)} %collective-permute-done.11.refs_1_, ...), custom_call_target="tpu_custom_call" | custom-call | tf_op jit(solution)/shard_map/pallas_call | solution.py:33
  105.9 3.1 %collective-permute-start.19 = (f32[4,1,128]{2,1,0:T(1,128)S(1)}, f32[4,1,128]{2,1,0:T(1,128)S(1)}, u32[]{:S(2)}, u32[]{:S(2)}) collective-permute-start(f32[4,1,128]{2,1,0:T(1,128)S(1)} %get-tuple-element.57), channel_id=1, source_target_pairs={{8,0},{16,8},{24,16},{32,24},{40,32},{48,40},{56,48},{0,56},{9,1},... | collective-permute-start | bytes 6152 | tf_op jit(solution)/shard_map/ppermute | solution.py:361
  114.6 3.4 %shard_map.111.refs_0_ = bf16[8,128,128]{2,1,0:T(8,128)(2,1)S(1)} custom-call(s32[16]{0:T(128)S(1)} %reshape.30.pick_ref, f32[32,128]{1,0:T(8,128)S(1)} %fusion.12.v_ref, bf16[512,4096]{1,0:T(8,128)(2,1)S(1)} %copy-done.2), custom_call_target="tpu_custom_call" | custom-call | tf_op jit(solution)/shard_map/pallas_call | solution.py:33
  123.5 3.0 %collective-permute-start.27 = (bf16[8,128,128]{2,1,0:T(8,128)(2,1)S(1)}, bf16[8,128,128]{2,1,0:T(8,128)(2,1)S(1)}, u32[]{:S(2)}, u32[]{:S(2)}) collective-permute-start(bf16[8,128,128]{2,1,0:T(8,128)(2,1)S(1)} %shard_map.111.refs_0_), channel_id=1, source_target_pairs={{0,8},{8,16},{16,24},{24,32},{32,40},{40,48},{48,56},{56,0},{1,9},... | collective-permute-start | bytes 786440 | tf_op jit(solution)/shard_map/ppermute | solution.py:347
  129.9 3.0 %collective-permute-done.28.refs_1_ = bf16[8,128,128]{2,1,0:T(8,128)(2,1)S(1)} collective-permute-done((bf16[8,128,128]{2,1,0:T(8,128)(2,1)S(1)}, bf16[8,128,128]{2,1,0:T(8,128)(2,1)S(1)}, u32[]{:S(2)}, u32[]{:S(2)}) %collective-permute-start.28) | collective-permute-done | bytes 262176 | tf_op jit(solution)/shard_map/ppermute | solution.py:348
  135.1 5.6 %all-to-all-start.2 = ((bf16[8,5,128,128]{3,2,1,0:T(8,128)(2,1)}), bf16[8,5,128,128]{3,2,1,0:T(8,128)(2,1)S(1)}, u32[]{:S(2)}, u32[]{:S(2)}) async-start(bf16[8,5,128,128]{3,2,1,0:T(8,128)(2,1)} %get-tuple-element.32), calls=%async_computation.2 | async-start | bytes 2621440 | tf_op jit(solution)/shard_map/all_to_all | solution.py:435
  147.4 10.1 %collective-permute-done.29.refs_1_ = bf16[3,128,128]{2,1,0:T(8,128)(2,1)S(1)} collective-permute-done((bf16[3,128,128]{2,1,0:T(8,128)(2,1)S(1)}, bf16[3,128,128]{2,1,0:T(8,128)(2,1)S(1)}, u32[]{:S(2)}, u32[]{:S(2)}) %collective-permute-start.29) | collective-permute-done | bytes 98336 | tf_op jit(solution)/shard_map/ppermute | solution.py:455
  163.2 3.5 %collective-permute-done.32.refs_4_ = bf16[3,128,128]{2,1,0:T(8,128)(2,1)S(1)} collective-permute-done((bf16[3,128,128]{2,1,0:T(8,128)(2,1)S(1)}, bf16[3,128,128]{2,1,0:T(8,128)(2,1)S(1)}, u32[]{:S(2)}, u32[]{:S(2)}) %collective-permute-start.32) | collective-permute-done | bytes 98336 | tf_op jit(solution)/shard_map/ppermute | solution.py:455
  171.9 5.1 %collective-permute-done.39 = bf16[8,128,128]{2,1,0:T(8,128)(2,1)S(1)} collective-permute-done((bf16[8,128,128]{2,1,0:T(8,128)(2,1)S(1)}, bf16[8,128,128]{2,1,0:T(8,128)(2,1)S(1)}, u32[]{:S(2)}, u32[]{:S(2)}) %collective-permute-start.39) | collective-permute-done | bytes 262176 | tf_op jit(solution)/shard_map/ppermute | solution.py:482
  178.3 3.1 %collective-permute-start.37 = (bf16[8,128,128]{2,1,0:T(8,128)(2,1)S(1)}, bf16[8,128,128]{2,1,0:T(8,128)(2,1)S(1)}, u32[]{:S(2)}, u32[]{:S(2)}) collective-permute-start(bf16[8,128,128]{2,1,0:T(8,128)(2,1)S(1)} %add_convert_fusion.4), channel_id=1, source_target_pairs={{0,7},{1,0},{2,1},{3,2},{4,3},{5,4},{6,5},{7,6},{8,15},{9,8},{10,9... | collective-permute-start | bytes 786440 | tf_op jit(solution)/shard_map/ppermute | solution.py:487
  181.4 4.6 %collective-permute-done.40 = bf16[8,128,128]{2,1,0:T(8,128)(2,1)S(1)} collective-permute-done((bf16[8,128,128]{2,1,0:T(8,128)(2,1)S(1)}, bf16[8,128,128]{2,1,0:T(8,128)(2,1)S(1)}, u32[]{:S(2)}, u32[]{:S(2)}) %collective-permute-start.40) | collective-permute-done | bytes 262176 | tf_op jit(solution)/shard_map/ppermute | solution.py:485
  190.2 3.8 %collective-permute-done.41 = bf16[8,128,128]{2,1,0:T(8,128)(2,1)S(1)} collective-permute-done((bf16[8,128,128]{2,1,0:T(8,128)(2,1)S(1)}, bf16[8,128,128]{2,1,0:T(8,128)(2,1)S(1)}, u32[]{:S(2)}, u32[]{:S(2)}) %collective-permute-start.41) | collective-permute-done | bytes 262176 | tf_op jit(solution)/shard_map/ppermute | solution.py:488
  194.8 6.3 %collective-permute-done.42 = bf16[8,128,128]{2,1,0:T(8,128)(2,1)S(1)} collective-permute-done((bf16[8,128,128]{2,1,0:T(8,128)(2,1)S(1)}, bf16[8,128,128]{2,1,0:T(8,128)(2,1)S(1)}, u32[]{:S(2)}, u32[]{:S(2)}) %collective-permute-start.42) | collective-permute-done | bytes 262176 | tf_op jit(solution)/shard_map/ppermute | solution.py:491
  (128 shorter events, 76.9 us)
Async XLA Ops:
  0.6 12.7 %collective-permute-start = (bf16[8,128,128]{2,1,0:T(8,128)(2,1)}, bf16[8,128,128]{2,1,0:T(8,128)(2,1)S(1)}, u32[]{:S(2)}, u32[]{:S(2)}) collective-permute-start(bf16[8,128,128]{2,1,0:T(8,128)(2,1)} %in_ref.1), channel_id=1, source_target_pairs={{0,1},{1,2},{2,3},{3,4},{4,5},{5,6},{6,7},{7,0},{8,9},{9,10},{10,1... | collective-permute-start | bytes 786440 | tf_op jit(solution)/shard_map/ppermute | solution.py:431
  3.2 10.2 %collective-permute-start.1 = (bf16[8,128,128]{2,1,0:T(8,128)(2,1)}, bf16[8,128,128]{2,1,0:T(8,128)(2,1)S(1)}, u32[]{:S(2)}, u32[]{:S(2)}) collective-permute-start(bf16[8,128,128]{2,1,0:T(8,128)(2,1)} %in_ref.1), channel_id=1, source_target_pairs={{0,7},{1,0},{2,1},{3,2},{4,3},{5,4},{6,5},{7,6},{8,15},{9,8},{10,9... | collective-permute-start | bytes 786440 | tf_op jit(solution)/shard_map/ppermute | solution.py:431
  21.2 19.3 %collective-permute-start.5 = (bf16[8,128,128]{2,1,0:T(8,128)(2,1)S(1)}, bf16[8,128,128]{2,1,0:T(8,128)(2,1)S(1)}, u32[]{:S(2)}, u32[]{:S(2)}) collective-permute-start(bf16[8,128,128]{2,1,0:T(8,128)(2,1)S(1)} %collective-permute-done.3.refs_4_), channel_id=1, source_target_pairs={{0,7},{1,0},{2,1},{3,2},{4,3},{5,4},{6,5},{7,6},{8,15},{9,8},{10,9... | collective-permute-start | bytes 786440 | tf_op jit(solution)/shard_map/ppermute | solution.py:431
  28.1 12.3 %collective-permute-start.6 = (bf16[8,128,128]{2,1,0:T(8,128)(2,1)S(1)}, bf16[8,128,128]{2,1,0:T(8,128)(2,1)S(1)}, u32[]{:S(2)}, u32[]{:S(2)}) collective-permute-start(bf16[8,128,128]{2,1,0:T(8,128)(2,1)S(1)} %collective-permute-done.4.refs_0_), channel_id=1, source_target_pairs={{0,1},{1,2},{2,3},{3,4},{4,5},{5,6},{6,7},{7,0},{8,9},{9,10},{10,1... | collective-permute-start | bytes 786440 | tf_op jit(solution)/shard_map/ppermute | solution.py:463
  29.5 11.0 %all-to-all-start = ((s32[8,1,8]{2,1,0:T(1,128)}), s32[8,1,8]{2,1,0:T(1,128)S(1)}, u32[]{:S(2)}, u32[]{:S(2)}) async-start(s32[8,1,8]{2,1,0:T(1,128)} %shard_map.104), calls=%async_computation | async-start | bytes 8192 | tf_op jit(solution)/shard_map/all_to_all | solution.py:507
  41.2 12.9 %collective-permute-start.7 = (bf16[12,128,128]{2,1,0:T(8,128)(2,1)S(1)}, bf16[12,128,128]{2,1,0:T(8,128)(2,1)S(1)}, u32[]{:S(2)}, u32[]{:S(2)}) collective-permute-start(bf16[12,128,128]{2,1,0:T(8,128)(2,1)S(1)} %get-tuple-element.26), channel_id=1, source_target_pairs={{0,8},{8,0},{16,24},{24,16},{32,40},{40,32},{48,56},{56,48},{1,9},... | collective-permute-start | bytes 1179656 | tf_op jit(solution)/shard_map/ppermute | solution.py:440
  49.4 30.7 %all-to-all-start.1 = ((bf16[8,5,128,128]{3,2,1,0:T(8,128)(2,1)}), bf16[8,5,128,128]{3,2,1,0:T(8,128)(2,1)S(1)}, u32[]{:S(2)}, u32[]{:S(2)}) async-start(bf16[8,5,128,128]{3,2,1,0:T(8,128)(2,1)} %shard_map.106), calls=%async_computation.1 | async-start | bytes 2621440 | tf_op jit(solution)/shard_map/all_to_all | solution.py:435
  54.1 20.4 %collective-permute-start.10 = (bf16[6,128,128]{2,1,0:T(8,128)(2,1)S(1)}, bf16[6,128,128]{2,1,0:T(8,128)(2,1)S(1)}, u32[]{:S(2)}, u32[]{:S(2)}) collective-permute-start(bf16[6,128,128]{2,1,0:T(8,128)(2,1)S(1)} %pad_maximum_fusion.3), channel_id=1, source_target_pairs={{0,48},{8,56},{16,0},{24,8},{32,16},{40,24},{48,32},{56,40},{1,49}... | collective-permute-start | bytes 589832 | tf_op jit(solution)/shard_map/ppermute | solution.py:446
  56.8 19.3 %collective-permute-start.9 = (bf16[6,128,128]{2,1,0:T(8,128)(2,1)S(1)}, bf16[6,128,128]{2,1,0:T(8,128)(2,1)S(1)}, u32[]{:S(2)}, u32[]{:S(2)}) collective-permute-start(bf16[6,128,128]{2,1,0:T(8,128)(2,1)S(1)} %pad_maximum_fusion.2), channel_id=1, source_target_pairs={{0,32},{8,40},{16,48},{24,56},{32,0},{40,8},{48,16},{56,24},{1,33}... | collective-permute-start | bytes 589832 | tf_op jit(solution)/shard_map/ppermute | solution.py:446
  57.5 22.7 %collective-permute-start.8 = (bf16[6,128,128]{2,1,0:T(8,128)(2,1)S(1)}, bf16[6,128,128]{2,1,0:T(8,128)(2,1)S(1)}, u32[]{:S(2)}, u32[]{:S(2)}) collective-permute-start(bf16[6,128,128]{2,1,0:T(8,128)(2,1)S(1)} %pad_maximum_fusion.1), channel_id=1, source_target_pairs={{0,16},{8,24},{16,32},{24,40},{32,48},{40,56},{48,0},{56,8},{1,17}... | collective-permute-start | bytes 589832 | tf_op jit(solution)/shard_map/ppermute | solution.py:446
  86.2 11.2 %collective-permute-start.12 = (bf16[7,128,128]{2,1,0:T(8,128)(2,1)S(1)}, bf16[7,128,128]{2,1,0:T(8,128)(2,1)S(1)}, u32[]{:S(2)}, u32[]{:S(2)}) collective-permute-start(bf16[7,128,128]{2,1,0:T(8,128)(2,1)S(1)} %shard_map.108.refs_0_), channel_id=1, source_target_pairs={{64,0},{128,64},{192,128},{0,192},{65,1},{129,65},{193,129},{1,193... | collective-permute-start | bytes 688136 | tf_op jit(solution)/shard_map/ppermute | solution.py:348
  87.6 9.7 %collective-permute-start.13 = (bf16[7,128,128]{2,1,0:T(8,128)(2,1)S(1)}, bf16[7,128,128]{2,1,0:T(8,128)(2,1)S(1)}, u32[]{:S(2)}, u32[]{:S(2)}) collective-permute-start(bf16[7,128,128]{2,1,0:T(8,128)(2,1)S(1)} %shard_map.108.refs_0_), channel_id=1, source_target_pairs={{0,8},{8,16},{16,24},{24,32},{32,40},{40,48},{48,56},{56,0},{1,9},... | collective-permute-start | bytes 688136 | tf_op jit(solution)/shard_map/ppermute | solution.py:347
  104.3 10.2 %collective-permute-start.17 = (f32[1,8,128]{2,1,0:T(8,128)S(1)}, f32[1,8,128]{2,1,0:T(8,128)S(1)}, u32[]{:S(2)}, u32[]{:S(2)}) collective-permute-start(f32[1,8,128]{2,1,0:T(8,128)S(1)} %get-tuple-element.55), channel_id=1, source_target_pairs={{64,0},{128,64},{192,128},{0,192},{65,1},{129,65},{193,129},{1,193... | collective-permute-start | bytes 12296 | tf_op jit(solution)/shard_map/ppermute | solution.py:361
  118.2 10.0 %collective-permute-start.24 = (bf16[8,128,128]{2,1,0:T(8,128)(2,1)S(1)}, bf16[8,128,128]{2,1,0:T(8,128)(2,1)S(1)}, u32[]{:S(2)}, u32[]{:S(2)}) collective-permute-start(bf16[8,128,128]{2,1,0:T(8,128)(2,1)S(1)} %shard_map.111.refs_0_), channel_id=1, source_target_pairs={{64,0},{128,64},{192,128},{0,192},{65,1},{129,65},{193,129},{1,193... | collective-permute-start | bytes 786440 | tf_op jit(solution)/shard_map/ppermute | solution.py:348
  135.1 42.1 %all-to-all-start.2 = ((bf16[8,5,128,128]{3,2,1,0:T(8,128)(2,1)}), bf16[8,5,128,128]{3,2,1,0:T(8,128)(2,1)S(1)}, u32[]{:S(2)}, u32[]{:S(2)}) async-start(bf16[8,5,128,128]{3,2,1,0:T(8,128)(2,1)} %get-tuple-element.32), calls=%async_computation.2 | async-start | bytes 2621440 | tf_op jit(solution)/shard_map/all_to_all | solution.py:435
  140.7 16.7 %collective-permute-start.29 = (bf16[3,128,128]{2,1,0:T(8,128)(2,1)S(1)}, bf16[3,128,128]{2,1,0:T(8,128)(2,1)S(1)}, u32[]{:S(2)}, u32[]{:S(2)}) collective-permute-start(bf16[3,128,128]{2,1,0:T(8,128)(2,1)S(1)} %get-tuple-element.37), channel_id=1, source_target_pairs={{0,8},{8,16},{16,24},{24,32},{32,40},{40,48},{48,56},{56,0},{1,9},... | collective-permute-start | bytes 294920 | tf_op jit(solution)/shard_map/ppermute | solution.py:455
  142.4 20.0 %collective-permute-start.30 = (bf16[3,128,128]{2,1,0:T(8,128)(2,1)S(1)}, bf16[3,128,128]{2,1,0:T(8,128)(2,1)S(1)}, u32[]{:S(2)}, u32[]{:S(2)}) collective-permute-start(bf16[3,128,128]{2,1,0:T(8,128)(2,1)S(1)} %get-tuple-element.38), channel_id=1, source_target_pairs={{0,16},{8,24},{16,32},{24,40},{32,48},{40,56},{48,0},{56,8},{1,17}... | collective-permute-start | bytes 294920 | tf_op jit(solution)/shard_map/ppermute | solution.py:455
  143.6 19.7 %collective-permute-start.31 = (bf16[3,128,128]{2,1,0:T(8,128)(2,1)S(1)}, bf16[3,128,128]{2,1,0:T(8,128)(2,1)S(1)}, u32[]{:S(2)}, u32[]{:S(2)}) collective-permute-start(bf16[3,128,128]{2,1,0:T(8,128)(2,1)S(1)} %get-tuple-element.39), channel_id=1, source_target_pairs={{0,24},{8,32},{16,40},{24,48},{32,56},{40,0},{48,8},{56,16},{1,25}... | collective-permute-start | bytes 294920 | tf_op jit(solution)/shard_map/ppermute | solution.py:455
  145.2 21.5 %collective-permute-start.32 = (bf16[3,128,128]{2,1,0:T(8,128)(2,1)S(1)}, bf16[3,128,128]{2,1,0:T(8,128)(2,1)S(1)}, u32[]{:S(2)}, u32[]{:S(2)}) collective-permute-start(bf16[3,128,128]{2,1,0:T(8,128)(2,1)S(1)} %get-tuple-element.40), channel_id=1, source_target_pairs={{0,32},{8,40},{16,48},{24,56},{32,0},{40,8},{48,16},{56,24},{1,33}... | collective-permute-start | bytes 294920 | tf_op jit(solution)/shard_map/ppermute | solution.py:455
  145.7 21.5 %collective-permute-start.33 = (bf16[3,128,128]{2,1,0:T(8,128)(2,1)S(1)}, bf16[3,128,128]{2,1,0:T(8,128)(2,1)S(1)}, u32[]{:S(2)}, u32[]{:S(2)}) collective-permute-start(bf16[3,128,128]{2,1,0:T(8,128)(2,1)S(1)} %get-tuple-element.41), channel_id=1, source_target_pairs={{0,40},{8,48},{16,56},{24,0},{32,8},{40,16},{48,24},{56,32},{1,41}... | collective-permute-start | bytes 294920 | tf_op jit(solution)/shard_map/ppermute | solution.py:455
  157.5 9.8 %collective-permute-start.34 = (bf16[3,128,128]{2,1,0:T(8,128)(2,1)S(1)}, bf16[3,128,128]{2,1,0:T(8,128)(2,1)S(1)}, u32[]{:S(2)}, u32[]{:S(2)}) collective-permute-start(bf16[3,128,128]{2,1,0:T(8,128)(2,1)S(1)} %get-tuple-element.42), channel_id=1, source_target_pairs={{0,48},{8,56},{16,0},{24,8},{32,16},{40,24},{48,32},{56,40},{1,49}... | collective-permute-start | bytes 294920 | tf_op jit(solution)/shard_map/ppermute | solution.py:455
  168.1 9.0 %collective-permute-start.39 = (bf16[8,128,128]{2,1,0:T(8,128)(2,1)S(1)}, bf16[8,128,128]{2,1,0:T(8,128)(2,1)S(1)}, u32[]{:S(2)}, u32[]{:S(2)}) collective-permute-start(bf16[8,128,128]{2,1,0:T(8,128)(2,1)S(1)} %convert_element_type.54), channel_id=1, source_target_pairs={{0,1},{1,2},{2,3},{3,4},{4,5},{5,6},{6,7},{7,0},{8,9},{9,10},{10,1... | collective-permute-start | bytes 786440 | tf_op jit(solution)/shard_map/ppermute | solution.py:482
  169.1 9.1 %collective-permute-start.36 = (bf16[8,128,128]{2,1,0:T(8,128)(2,1)S(1)}, bf16[8,128,128]{2,1,0:T(8,128)(2,1)S(1)}, u32[]{:S(2)}, u32[]{:S(2)}) collective-permute-start(bf16[8,128,128]{2,1,0:T(8,128)(2,1)S(1)} %convert_element_type.48), channel_id=1, source_target_pairs={{0,7},{1,0},{2,1},{3,2},{4,3},{5,4},{6,5},{7,6},{8,15},{9,8},{10,9... | collective-permute-start | bytes 786440 | tf_op jit(solution)/shard_map/ppermute | solution.py:484
  178.3 9.0 %collective-permute-start.37 = (bf16[8,128,128]{2,1,0:T(8,128)(2,1)S(1)}, bf16[8,128,128]{2,1,0:T(8,128)(2,1)S(1)}, u32[]{:S(2)}, u32[]{:S(2)}) collective-permute-start(bf16[8,128,128]{2,1,0:T(8,128)(2,1)S(1)} %add_convert_fusion.4), channel_id=1, source_target_pairs={{0,7},{1,0},{2,1},{3,2},{4,3},{5,4},{6,5},{7,6},{8,15},{9,8},{10,9... | collective-permute-start | bytes 786440 | tf_op jit(solution)/shard_map/ppermute | solution.py:487
  (33 other events, 264.5 us)
